TPU v7x, 32 devices: a whole 2x2x4 slice. The times are simulated.
32 devices in a mesh: dp: 4 (over y, x), row: 4 (over z), col: 2 (over core).
Axes of the slice: x: 2, y: 2, z: 4, core: 2. Of those that a mesh axis runs over, the one named last changes fastest.
Arguments:
- block_input: bfloat16 [192, 197, 384], P(('dp', 'row', 'col')), may hold values from -6 to 6
- first_norm_scale: float32 [384], P('row'), may hold values from 0.5 to 1.5
- first_norm_bias: float32 [384], P('row'), may hold values from -1.5 to 1.5
- attn_weight: bfloat16 [6, 384, 256], P('col', 'row'), may hold values from -1.2247449 to 1.2247449
- qv_bias: float32 [2, 384], P(None, 'col'), may hold values from -2.5 to 2.5
- out_bias: float32 [384], P('row'), may hold values from -2.5 to 2.5
- second_norm_scale: float32 [384], P('row'), may hold values from 0.5 to 1.5
- second_norm_bias: float32 [384], P('row'), may hold values from -1.5 to 1.5
- up_weight: bfloat16 [384, 1536], P('row', 'col'), may hold values from -0.3125 to 0.3125
- up_bias: float32 [1536], P('col'), may hold values from -2.5 to 2.5
- down_weight: bfloat16 [384, 1536], P('row', 'col'), may hold values from -0.15625 to 0.15625
- down_bias: float32 [384], P('row'), may hold values from -2.5 to 2.5
- cotangent: bfloat16 [192, 197, 384], P(('dp', 'row', 'col')), may hold values from -6 to 6
Outputs:
- block_output: bfloat16 [192, 197, 384], P(('dp', 'row', 'col'))
- d_x: float32 [192, 197, 384], P(('dp', 'row', 'col'))
- d_ln1_gain: float32 [384], P('row')
- d_ln1_shift: float32 [384], P('row')
- d_attn_weight: float32 [6, 384, 256], P('col', 'row')
- d_qv_bias: float32 [2, 384], P(None, 'col')
- d_out_bias: float32 [384], P('row')
- d_ln2_gain: float32 [384], P('row')
- d_ln2_shift: float32 [384], P('row')
- d_up_weight: float32 [384, 1536], P('row', 'col')
- d_up_bias: float32 [1536], P('col')
- d_down_weight: float32 [384, 1536], P('row', 'col')
- d_down_bias: float32 [384], P('row')
All inputs are finite; a program needn't handle non-finite values.
Results may differ from a plain program's by a relative error of at most 0.013.
Values may be sent and summed in bfloat16 or wider, within the bound.
A program may use at most 448 MiB of HBM per device.

v0:
```python
import math

import jax
import jax.numpy as jnp
from jax import lax
from jax.sharding import PartitionSpec as P

SEQ = 197
HD = 64


EPS = 1e-06
ROOT_HALF = 0.7071067811865476
INV_ROOT_TWO_PI = 0.3989422804014327


def gelu_parts(u):
    cdf = 0.5 * (1.0 + jax.scipy.special.erf(u * ROOT_HALF))
    return (u * cdf, cdf + u * jnp.exp(-0.5 * u * u) * INV_ROOT_TWO_PI)


def row_sum_values(pair):
    return lax.psum((pair[0], pair[1]), "row")


def layer_norm_forward(input_value, scale_factor, offset_bias, feature_width):
    partial_sum_values = row_sum_values(
        (jnp.sum(input_value, -1), jnp.sum(input_value * input_value, -1))
    )
    row_average = partial_sum_values[0] / feature_width
    var = partial_sum_values[1] / feature_width - row_average * row_average
    inverse_deviation = lax.rsqrt(var + EPS)[..., None]
    normalized_input = (input_value - row_average[..., None]) * inverse_deviation
    return (
        normalized_input,
        inverse_deviation,
        (normalized_input * scale_factor + offset_bias).astype(jnp.bfloat16),
    )


def layer_norm_backward(
    incoming_gradient, normalized_input, inverse_deviation, scale_factor, feature_width
):
    normalized_gradient = incoming_gradient * scale_factor
    partial_sum_values = row_sum_values(
        (jnp.sum(normalized_gradient, -1), jnp.sum(normalized_gradient * normalized_input, -1))
    )
    return inverse_deviation * (
        normalized_gradient
        - partial_sum_values[0][..., None] / feature_width
        - normalized_input * (partial_sum_values[1][..., None] / feature_width)
    )


def gather_cols(values):
    return lax.all_gather(values, "col", axis=0, tiled=True)


def gather_rows(values):
    return lax.all_gather(values, "row", axis=0, tiled=True)


def project_in(whole_rows, weight):
    mine = lax.all_to_all(whole_rows, "row", split_axis=0, concat_axis=2, tiled=True)
    full_weight = lax.all_gather(weight, "row", axis=0, tiled=True)
    return jnp.dot(mine, full_weight, preferred_element_type=jnp.float32)


def project_out(whole_rows, weight):
    return lax.psum_scatter(
        jnp.dot(whole_rows, weight, preferred_element_type=jnp.float32),
        "col",
        scatter_dimension=0,
        tiled=True,
    )


def back_to_middle(whole_grad, weight):
    mine = lax.all_to_all(whole_grad, "row", split_axis=0, concat_axis=2, tiled=True)
    full_weight = lax.all_gather(weight, "row", axis=1, tiled=True)
    return lax.dot_general(
        mine, full_weight, (((2,), (1,)), ((), ())), preferred_element_type=jnp.float32
    )


def back_to_input(whole_grad, weight):
    return lax.psum_scatter(
        lax.dot_general(
            whole_grad, weight, (((2,), (1,)), ((), ())), preferred_element_type=jnp.float32
        ),
        "col",
        scatter_dimension=0,
        tiled=True,
    )


def token_product(left, incoming_gradient):
    return lax.dot_general(
        left, incoming_gradient, (((0, 1), (0, 1)), ((), ())), preferred_element_type=jnp.float32
    )


def token_sum(incoming_gradient):
    return jnp.sum(incoming_gradient, axis=(0, 1), dtype=jnp.float32)


def sum_weights(grads):
    return (
        lax.psum(grads[0].astype(jnp.bfloat16), "dp").astype(jnp.float32),
        lax.psum(grads[1].astype(jnp.bfloat16), "dp").astype(jnp.float32),
        lax.psum(grads[2].astype(jnp.bfloat16), "dp").astype(jnp.float32),
        lax.psum(grads[3].astype(jnp.bfloat16), "dp").astype(jnp.float32),
        lax.psum(grads[4].astype(jnp.bfloat16), "dp").astype(jnp.float32),
        lax.psum(grads[5].astype(jnp.bfloat16), "dp").astype(jnp.float32),
        lax.psum(grads[6].astype(jnp.bfloat16), "dp").astype(jnp.float32),
    )


def sum_norms(grads):
    return lax.psum((grads[0], grads[1], grads[2], grads[3]), ("dp", "col"))


def attend_block(inputs):
    query, keys, values = inputs
    scale = 1.0 / math.sqrt(query.shape[-1])
    scores = jnp.einsum("bqhd,bkhd->bhqk", query, keys, preferred_element_type=jnp.float32) * scale
    top = jnp.max(scores, -1, keepdims=True)
    lse = top + jnp.log(jnp.sum(jnp.exp(scores - top), -1, keepdims=True))
    probs = jnp.exp(scores - lse).astype(jnp.bfloat16)
    out = jnp.einsum("bhqk,bkhd->bqhd", probs, values, preferred_element_type=jnp.float32)
    return (out.astype(jnp.bfloat16), lse)


def attend_back_block(inputs):
    query, keys, values, lse, dout = inputs
    scale = 1.0 / math.sqrt(query.shape[-1])
    scores = jnp.einsum("bqhd,bkhd->bhqk", query, keys, preferred_element_type=jnp.float32) * scale
    probs = jnp.exp(scores - lse)
    probs_b = probs.astype(jnp.bfloat16)
    dvals = jnp.einsum("bhqk,bqhd->bkhd", probs_b, dout, preferred_element_type=jnp.float32)
    dprob = jnp.einsum("bqhd,bkhd->bhqk", dout, values, preferred_element_type=jnp.float32)
    delta = jnp.sum(probs * dprob, -1, keepdims=True)
    dsb = (probs * (dprob - delta)).astype(jnp.bfloat16)
    dquery = jnp.einsum("bhqk,bkhd->bqhd", dsb, keys, preferred_element_type=jnp.float32) * scale
    dkeys = jnp.einsum("bhqk,bqhd->bkhd", dsb, query, preferred_element_type=jnp.float32) * scale
    return (dquery.astype(jnp.bfloat16), dkeys.astype(jnp.bfloat16), dvals.astype(jnp.bfloat16))


def local(
    block_input,
    first_norm_scale,
    first_norm_bias,
    attn_weight,
    qv_bias,
    out_bias,
    second_norm_scale,
    second_norm_bias,
    up_weight,
    up_bias,
    down_weight,
    down_bias,
    cotangent,
):
    split_input, split_cotangent = (
        lax.all_to_all(block_input, "row", split_axis=2, concat_axis=0, tiled=True),
        lax.all_to_all(cotangent, "row", split_axis=2, concat_axis=0, tiled=True),
    )
    head_count = attn_weight.shape[0]
    feat_rows = attn_weight.shape[1]
    feat_cols = head_count * HD
    feature_width = feat_rows * lax.axis_size("row")
    qkv_local = (
        attn_weight[:, :, : 3 * HD]
        .reshape(head_count, feat_rows, 3, HD)
        .transpose(1, 2, 0, 3)
        .reshape(feat_rows, 3 * feat_cols)
    )
    out_local = attn_weight[:, :, 3 * HD :].transpose(0, 2, 1).reshape(feat_cols, feat_rows)
    down_local = down_weight.T
    input_as_float = split_input.astype(jnp.float32)
    first_normalized_input, first_inverse_deviation, first_normed_output = layer_norm_forward(
        input_as_float, first_norm_scale, first_norm_bias, feature_width
    )
    whole1 = gather_cols(first_normed_output)
    qkv = project_in(whole1, qkv_local)
    images_mine = qkv.shape[0]
    bias_three = jnp.stack([qv_bias[0], jnp.zeros_like(qv_bias[0]), qv_bias[1]])
    qkv = qkv.reshape(images_mine, SEQ, 3, feat_cols) + bias_three
    group = math.gcd(images_mine, 6)
    nblocks = images_mine // group
    split_shape = (nblocks, group, SEQ, head_count, HD)
    query = qkv[:, :, 0].astype(jnp.bfloat16).reshape(split_shape)
    keys = qkv[:, :, 1].astype(jnp.bfloat16).reshape(split_shape)
    values = qkv[:, :, 2].astype(jnp.bfloat16).reshape(split_shape)
    attn, lse = lax.map(attend_block, (query, keys, values))
    attn_flat = attn.reshape(images_mine, SEQ, feat_cols)
    attn_whole = gather_rows(attn_flat)
    hidden_input = input_as_float + project_out(attn_whole, out_local) + out_bias
    second_normalized_input, second_inverse_deviation, second_normed_output = layer_norm_forward(
        hidden_input, second_norm_scale, second_norm_bias, feature_width
    )
    whole2 = gather_cols(second_normed_output)
    pre = project_in(whole2, up_weight) + up_bias
    act, slope = gelu_parts(pre)
    act_b = act.astype(jnp.bfloat16)
    act_whole = gather_rows(act_b)
    y_out = (hidden_input + project_out(act_whole, down_local) + down_bias).astype(jnp.bfloat16)
    grad_whole = gather_cols(split_cotangent)
    g_down_w = token_product(grad_whole, act_whole)
    g_down_b = token_sum(grad_whole)
    dpre = (back_to_middle(grad_whole, down_local) * slope).astype(jnp.bfloat16)
    dpre_whole = gather_rows(dpre)
    g_up_w = token_product(whole2, dpre_whole)
    g_up_b = token_sum(dpre_whole)
    second_activation_grad = back_to_input(dpre_whole, up_weight)
    second_norm_scale_grad = jnp.sum(second_activation_grad * second_normalized_input, (0, 1))
    g_ln2_s = jnp.sum(second_activation_grad, (0, 1))
    hidden_gradient = split_cotangent.astype(jnp.float32) + layer_norm_backward(
        second_activation_grad,
        second_normalized_input,
        second_inverse_deviation,
        second_norm_scale,
        feature_width,
    )
    dhb = hidden_gradient.astype(jnp.bfloat16)
    dh_whole = gather_cols(dhb)
    g_out_w = token_product(attn_whole, dh_whole)
    g_out_b = token_sum(dh_whole)
    dout = back_to_middle(dh_whole, out_local).astype(jnp.bfloat16).reshape(split_shape)
    dquery, dkeys, dvals = lax.map(attend_back_block, (query, keys, values, lse, dout))
    dqkv = jnp.stack(
        [
            dquery.reshape(images_mine, SEQ, feat_cols),
            dkeys.reshape(images_mine, SEQ, feat_cols),
            dvals.reshape(images_mine, SEQ, feat_cols),
        ],
        2,
    ).reshape(images_mine, SEQ, 3 * feat_cols)
    dqkv_whole = gather_rows(dqkv)
    g_qkv_w = token_product(whole1, dqkv_whole)
    bias_sums = token_sum(dqkv_whole).reshape(3, feat_cols)
    g_qv_b = jnp.stack([bias_sums[0], bias_sums[2]])
    packed_qkv = (
        g_qkv_w.reshape(feat_rows, 3, head_count, HD)
        .transpose(2, 0, 1, 3)
        .reshape(head_count, feat_rows, 3 * HD)
    )
    packed_out = g_out_w.reshape(head_count, HD, feat_rows).transpose(0, 2, 1)
    g_attn = jnp.concatenate([packed_qkv, packed_out], 2)
    first_activation_grad = back_to_input(dqkv_whole, qkv_local)
    first_norm_scale_grad = jnp.sum(first_activation_grad * first_normalized_input, (0, 1))
    g_ln1_s = jnp.sum(first_activation_grad, (0, 1))
    output_input_gradient = hidden_gradient + layer_norm_backward(
        first_activation_grad,
        first_normalized_input,
        first_inverse_deviation,
        first_norm_scale,
        feature_width,
    )
    totals = sum_weights((g_attn, g_qv_b, g_out_b, g_up_w, g_up_b, g_down_w, g_down_b))
    norms = sum_norms((first_norm_scale_grad, g_ln1_s, second_norm_scale_grad, g_ln2_s))
    y_back, dx_back = (
        lax.all_to_all(
            y_out.astype(jnp.float32).astype(jnp.bfloat16),
            "row",
            split_axis=0,
            concat_axis=2,
            tiled=True,
        ).astype(jnp.float32),
        lax.all_to_all(
            output_input_gradient.astype(jnp.bfloat16),
            "row",
            split_axis=0,
            concat_axis=2,
            tiled=True,
        ).astype(output_input_gradient.dtype),
    )
    return (
        y_back.astype(jnp.bfloat16),
        dx_back,
        norms[0],
        norms[1],
        totals[0],
        totals[1],
        totals[2],
        norms[2],
        norms[3],
        totals[3],
        totals[4],
        totals[5],
        totals[6],
    )


def solution(mesh):
    placed = (
        P(("dp", "row", "col"), None, None),
        P("row"),
        P("row"),
        P("col", "row", None),
        P(None, "col"),
        P("row"),
        P("row"),
        P("row"),
        P("row", "col"),
        P("col"),
        P("row", "col"),
        P("row"),
        P(("dp", "row", "col"), None, None),
    )
    return jax.shard_map(
        local,
        mesh=mesh,
        in_specs=placed,
        out_specs=(
            P(("dp", "row", "col"), None, None),
            P(("dp", "row", "col"), None, None),
            P("row"),
            P("row"),
            P("col", "row", None),
            P(None, "col"),
            P("row"),
            P("row"),
            P("row"),
            P("row", "col"),
            P("col"),
            P("row", "col"),
            P("row"),
        ),
        check_vma=False,
    )
```

profile of v0, /device:TPU:0, one launch (start us, length us, event | category | flops | bytes accessed | tf_op | source)
XLA Modules:
  0.0 1589.5 jit_solution(12312043903524667726)
XLA Ops:
  9.5 43.1 %all_to_all.126 = bf16[6,197,384]{1,0,2:T(8,128)(2,1)S(1)} all-to-all(bf16[6,197,384]{1,0,2:T(8,128)(2,1)S(1)} %copy.109), channel_id=1, replica_groups=mesh['dp'=4,'row'=4,'col'=2] {'row'}, dimensions={2} | all-to-all | bytes 1815552 | tf_op jit(solution)/shard_map/all_to_all | solution.py:165
  62.7 17.6 %all-reduce.4 = (f32[24,197]{1,0:T(8,128)S(1)}, f32[24,197]{1,0:T(8,128)S(1)}) all-reduce(f32[24,197]{1,0:T(8,128)S(1)} %reduce_sum.178, f32[24,197]{1,0:T(8,128)S(1)} %reduce_sum.176), channel_id=1, replica_groups=mesh['dp'=4,'row'=4,'col'=2] {'row'}, use_global_device_ids=true, to_apply=%region_3.0 | all-reduce | flops 9456 | bytes 75648 | tf_op jit(solution)/shard_map/psum | solution.py:23
  97.8 63.3 %all_gather.37 = bf16[384,576]{1,0:T(8,128)(2,1)S(1)} all-gather(bf16[96,576]{1,0:T(8,128)(2,1)S(1)} %copy.117), channel_id=1, replica_groups=mesh['dp'=4,'row'=4,'col'=2] {'row'}, dimensions={0}, use_global_device_ids=true | all-gather | bytes 552960 | tf_op jit(solution)/shard_map/all_gather | solution.py:65
  187.5 80.7 %all_to_all.127 = bf16[6,197,384]{1,0,2:T(8,128)(2,1)} all-to-all(bf16[6,197,384]{1,0,2:T(8,128)(2,1)} %copy.123), channel_id=1, replica_groups=mesh['dp'=4,'row'=4,'col'=2] {'row'}, dimensions={2} | all-to-all | bytes 1815552 | tf_op jit(solution)/shard_map/all_to_all | solution.py:166
  278.1 24.4 %all-gather.11.cloned.1.call-done = bf16[48,197,192]{1,2,0:T(8,128)(2,1)} async-done(((bf16[12,197,192]{1,2,0:T(8,128)(2,1)}), bf16[48,197,192]{1,2,0:T(8,128)(2,1)}) %all-gather.11.cloned.1.call-update) | async-done | bytes 3631120 | tf_op jit(solution)/shard_map/all_gather | solution.py:60
  319.1 11.0 reduce-scatter.5.cloned.1.call-done
  335.2 48.0 %all-reduce.3 = (f32[24,197]{1,0:T(8,128)}, f32[24,197]{1,0:T(8,128)}) all-reduce(f32[24,197]{1,0:T(8,128)} %get-tuple-element.150, f32[24,197]{1,0:T(8,128)} %get-tuple-element.149), channel_id=1, replica_groups=mesh['dp'=4,'row'=4,'col'=2] {'row'}, use_global_device_ids=true, to_apply=%region_12.13 | all-reduce | flops 9456 | bytes 75648 | tf_op jit(solution)/shard_map/psum | solution.py:23
  387.8 11.2 all-gather.13.cloned.1.call-done
  403.9 65.9 %all_gather.43 = bf16[768,384]{0,1:T(8,128)(2,1)} all-gather(bf16[768,96]{0,1:T(8,128)(2,1)} %bitcast.266), channel_id=1, replica_groups=mesh['dp'=4,'row'=4,'col'=2] {'row'}, dimensions={1}, use_global_device_ids=true | all-gather | bytes 737280 | tf_op jit(solution)/shard_map/all_gather | solution.py:80
  469.8 17.0 %all_gather.40 = bf16[384,768]{1,0:T(8,128)(2,1)} all-gather(bf16[96,768]{1,0:T(8,128)(2,1)} %param.25), channel_id=1, replica_groups=mesh['dp'=4,'row'=4,'col'=2] {'row'}, dimensions={0}, use_global_device_ids=true | all-gather | bytes 737280 | tf_op jit(solution)/shard_map/all_gather | solution.py:65
  518.9 254.0 %all-gather.19.cloned.1.call-done = bf16[48,197,768]{2,1,0:T(8,128)(2,1)} async-done(((bf16[12,197,768]{2,1,0:T(8,128)(2,1)}), bf16[48,197,768]{2,1,0:T(8,128)(2,1)}) %all-gather.19.cloned.1.call-update) | async-done | bytes 14524432 | tf_op jit(solution)/shard_map/all_gather | solution.py:60
  782.4 10.8 reduce-scatter.9.cloned.1.call-done
  797.4 21.0 %all-reduce.2 = (f32[24,197]{1,0:T(8,128)}, f32[24,197]{1,0:T(8,128)}) all-reduce(f32[24,197]{1,0:T(8,128)} %get-tuple-element.140, f32[24,197]{1,0:T(8,128)} %get-tuple-element.146), channel_id=1, replica_groups=mesh['dp'=4,'row'=4,'col'=2] {'row'}, use_global_device_ids=true, to_apply=%region_18.19 | all-reduce | flops 9456 | bytes 75648 | tf_op jit(solution)/shard_map/psum | solution.py:23
  840.2 60.5 %all_gather.46 = bf16[192,384]{0,1:T(8,128)(2,1)} all-gather(bf16[192,96]{0,1:T(8,128)(2,1)} %copy.128), channel_id=1, replica_groups=mesh['dp'=4,'row'=4,'col'=2] {'row'}, dimensions={1}, use_global_device_ids=true | all-gather | bytes 184320 | tf_op jit(solution)/shard_map/all_gather | solution.py:80
  918.5 17.9 %while.27 = (s32[]{:T(128)}, bf16[2,6,197,3,64]{2,4,3,1,0:T(8,128)(2,1)}, bf16[2,6,197,3,64]{2,4,3,1,0:T(8,128)(2,1)}, bf16[2,6,197,3,64]{2,4,3,1,0:T(8,128)(2,1...) while((s32[]{:T(128)}, ...), condition=%wide.region_21.22_spmd, body=%wide.region_19.21_spmd.sunk | while | flops 456593600 | bytes 55074784 | solution.py:230
  943.1 213.1 %all-gather.23.cloned.1.call-done = bf16[48,197,576]{2,1,0:T(8,128)(2,1)} async-done(((bf16[12,197,576]{2,1,0:T(8,128)(2,1)}), bf16[48,197,576]{2,1,0:T(8,128)(2,1)}) %all-gather.23.cloned.1.call-update) | async-done | bytes 10893328 | tf_op jit(solution)/shard_map/all_gather | solution.py:60
  1156.2 11.7 fusion.87
  1168.2 241.2 %all-gather.15.cloned.1.call-done = bf16[48,197,768]{2,1,0:T(8,128)(2,1)} async-done(((bf16[12,197,768]{2,1,0:T(8,128)(2,1)}), bf16[48,197,768]{2,1,0:T(8,128)(2,1)}) %all-gather.15.cloned.1.call-update) | async-done | bytes 14524432 | tf_op jit(solution)/shard_map/all_gather | solution.py:60
  1409.4 11.9 fusion.78
  1436.1 18.1 %all-reduce.1 = (f32[24,197]{1,0:T(8,128)}, f32[24,197]{1,0:T(8,128)}) all-reduce(f32[24,197]{1,0:T(8,128)} %get-tuple-element.142, f32[24,197]{1,0:T(8,128)} %get-tuple-element.145), channel_id=1, replica_groups=mesh['dp'=4,'row'=4,'col'=2] {'row'}, use_global_device_ids=true, to_apply=%region_26.27 | all-reduce | flops 9456 | bytes 75648 | tf_op jit(solution)/shard_map/psum | solution.py:23
  1480.4 12.8 all-to-all-done.3
  1526.9 10.0 all-reduce.5
  1539.1 17.3 %all-reduce.9.cloned.1.call-done = (bf16[3,96,256]{1,2,0:T(8,128)(2,1)}, bf16[96,768]{1,0:T(8,128)(2,1)}, bf16[96,768]{1,0:T(8,128)(2,1)}) async-done(((bf16[3,96,256]{1,2,0:T(8,128)(2,1)}, bf16[96,768]{1,0:T(8,128)(2,1)}, bf16[96,768]{1,0:T(8,128)(2,1)}), (bf16[3,96,256]{1,2,0:T(8,128)(2,1)}, bf16[96,768]{1,0:T(8,128)(2,1)}, bf16[96,768]{1,0:T(8,128)(2,1)})) %all-reduce.9.cloned.1.call-update) | async-done | bytes 442384 | tf_op jit(solution)/shard_map/psum | solution.py:109
  1561.5 12.6 all-reduce
  (253 shorter events, 305.1 us)
Async XLA Ops:
  7.2 84.7 %all-gather.9.cloned.1.call-start = ((), (), s32[]{:S(2)}) async-start(), calls=%async_computation.12 | async-start | bytes 3538944 | tf_op jit(solution)/shard_map/all_gather | solution.py:56
  91.9 69.6 %all-to-all-start.1 = ((bf16[48,197,96]{1,2,0:T(8,128)(2,1)}), bf16[48,197,96]{1,2,0:T(8,128)(2,1)S(1)}, u32[]{:S(2)}, u32[]{:S(2)}) async-start(bf16[48,197,96]{1,2,0:T(8,128)(2,1)} %all-gather.9.cloned.1.call-done), calls=%async_computation.1 | async-start | bytes 4718592 | tf_op jit(solution)/shard_map/all_to_all | solution.py:64
  96.7 64.6 %copy-start.35 = (f32[2,192]{1,0:T(2,128)S(1)}, f32[2,192]{1,0:T(2,128)}, u32[]{:S(2)}) copy-start(f32[2,192]{1,0:T(2,128)} %param.21) | copy-start | bytes 4612
  96.7 205.8 %all-gather.11.cloned.1.call-start = ((), (), s32[]{:S(2)}) async-start(), calls=%async_computation.13 | async-start | bytes 5898240 | tf_op jit(solution)/shard_map/all_gather | solution.py:60
  184.1 130.1 %all-gather.17.cloned.1.call-start = ((), (), s32[]{:S(2)}) async-start(), calls=%async_computation.18 | async-start | bytes 3538944 | tf_op jit(solution)/shard_map/all_gather | solution.py:56
  274.9 55.3 %reduce-scatter.5.cloned.1.call-start = ((), (), s32[]{:S(2)}) async-start(), calls=%async_computation.14 | async-start | bytes 7077888 | tf_op jit(solution)/shard_map/reduce_scatter | solution.py:70
  314.2 73.6 %all-to-all-start.5 = ((bf16[48,197,96]{1,2,0:T(8,128)(2,1)}), bf16[48,197,96]{1,2,0:T(8,128)(2,1)}, u32[]{:S(2)}, u32[]{:S(2)}) async-start(bf16[48,197,96]{1,2,0:T(8,128)(2,1)} %all-gather.17.cloned.1.call-done), calls=%async_computation.7 | async-start | bytes 4718592 | tf_op jit(solution)/shard_map/all_to_all | solution.py:79
  319.1 65.5 %copy-start.30 = (f32[96]{0:T(128)S(1)}, f32[96]{0:T(128)}, u32[]{:S(2)}) copy-start(f32[96]{0:T(128)} %param.23) | copy-start | bytes 1156
  319.1 65.5 %copy-start.40 = (f32[96]{0:T(128)S(1)}, f32[96]{0:T(128)}, u32[]{:S(2)}) copy-start(f32[96]{0:T(128)} %param.24) | copy-start | bytes 1156
  319.1 80.0 %all-gather.13.cloned.1.call-start = ((), (), s32[]{:S(2)}) async-start(), calls=%async_computation.15 | async-start | bytes 3538944 | tf_op jit(solution)/shard_map/all_gather | solution.py:56
  399.1 98.6 %all-to-all-start.2 = ((bf16[48,197,96]{1,2,0:T(8,128)(2,1)}), bf16[48,197,96]{1,2,0:T(8,128)(2,1)}, u32[]{:S(2)}, u32[]{:S(2)}) async-start(bf16[48,197,96]{1,2,0:T(8,128)(2,1)} %all-gather.13.cloned.1.call-done), calls=%async_computation.3 | async-start | bytes 4718592 | tf_op jit(solution)/shard_map/all_to_all | solution.py:64
  403.9 368.9 %all-gather.19.cloned.1.call-start = ((), (), s32[]{:S(2)}) async-start(), calls=%async_computation.19 | async-start | bytes 18432000 | tf_op jit(solution)/shard_map/all_gather | solution.py:60
  518.8 274.4 %reduce-scatter.9.cloned.1.call-start = ((), (), s32[]{:S(2)}) async-start(), calls=%async_computation.20 | async-start | bytes 7077888 | tf_op jit(solution)/shard_map/reduce_scatter | solution.py:87
  782.4 51.5 %all-gather.21.cloned.1.call-start = ((), (), s32[]{:S(2)}) async-start(), calls=%async_computation.21 | async-start | bytes 3538944 | tf_op jit(solution)/shard_map/all_gather | solution.py:56
  833.9 66.9 %all-to-all-start.6 = ((bf16[48,197,96]{1,2,0:T(8,128)(2,1)}), bf16[48,197,96]{1,2,0:T(8,128)(2,1)}, u32[]{:S(2)}, u32[]{:S(2)}) async-start(bf16[48,197,96]{1,2,0:T(8,128)(2,1)} %all-gather.21.cloned.1.call-done), calls=%async_computation.9 | async-start | bytes 4718592 | tf_op jit(solution)/shard_map/all_to_all | solution.py:79
  838.7 317.5 %all-gather.23.cloned.1.call-start = ((), (), s32[]{:S(2)}) async-start(), calls=%async_computation.22 | async-start | bytes 15360000 | tf_op jit(solution)/shard_map/all_gather | solution.py:60
  942.5 213.7 %copy-start.18 = (bf16[96,3,3,64]{0,3,2,1:T(8,128)(2,1)S(1)}, bf16[96,3,3,64]{0,3,2,1:T(8,128)(2,1)}, u32[]{:S(2)}) copy-start(bf16[96,3,3,64]{0,3,2,1:T(8,128)(2,1)} %copy-done.17) | copy-start | bytes 331780
  942.5 466.9 %all-gather.15.cloned.1.call-start = ((), (), s32[]{:S(2)}) async-start(), calls=%async_computation.16 | async-start | bytes 18432000 | tf_op jit(solution)/shard_map/all_gather | solution.py:60
  943.1 488.5 %reduce-scatter.11.cloned.1.call-start = ((), (), s32[]{:S(2)}) async-start(), calls=%async_computation.23 | async-start | bytes 7077888 | tf_op jit(solution)/shard_map/reduce_scatter | solution.py:87
  1167.9 241.5 %copy-start.22 = (bf16[96,768]{1,0:T(8,128)(2,1)S(1)}, bf16[96,768]{1,0:T(8,128)(2,1)}, u32[]{:S(2)}) copy-start(bf16[96,768]{1,0:T(8,128)(2,1)} %param.27) | copy-start | bytes 442372
  1167.9 289.0 %reduce-scatter.7.cloned.1.call-start = ((), (), s32[]{:S(2)}) async-start(), calls=%async_computation.17 | async-start | bytes 7077888 | tf_op jit(solution)/shard_map/reduce_scatter | solution.py:70
  1464.4 28.8 %all-to-all-start.3 = ((bf16[24,197,96]{1,2,0:T(8,128)(2,1)}), bf16[24,197,96]{1,2,0:T(8,128)(2,1)S(1)}, u32[]{:S(2)}, u32[]{:S(2)}) async-start(bf16[24,197,96]{1,2,0:T(8,128)(2,1)} %get-tuple-element.211), calls=%async_computation.5 | async-start | bytes 2359296 | tf_op jit(solution)/shard_map/all_to_all | solution.py:263
  1493.2 84.3 %all-to-all-start.7 = ((bf16[24,197,96]{1,2,0:T(8,128)(2,1)}), bf16[24,197,96]{1,2,0:T(8,128)(2,1)}, u32[]{:S(2)}, u32[]{:S(2)}) async-start(bf16[24,197,96]{1,2,0:T(8,128)(2,1)} %get-tuple-element.210), calls=%async_computation.11 | async-start | bytes 2359296 | tf_op jit(solution)/shard_map/all_to_all | solution.py:270
  1497.5 59.0 %all-reduce.9.cloned.1.call-start = ((), (), s32[]{:S(2)}) async-start(), calls=%async_computation.24 | async-start | bytes 983040 | tf_op jit(solution)/shard_map/psum | solution.py:109
  (48 other events, 316.5 us)
Sparse Core Ops, SparseCore 0:
  82.6 9.1 all-gather.8
  184.2 118.2 all-gather.10
  304.1 10.0 all-gather.16
  316.4 13.7 reduce-scatter.4
  388.0 11.0 all-gather.12
  519.0 253.8 all-gather.18
  782.5 10.7 reduce-scatter.8
  824.7 9.1 all-gather.20
  942.6 213.5 all-gather.22
  1157.6 251.7 all-gather.14
  1411.7 10.7 reduce-scatter.10
  1424.6 13.8 reduce-scatter.6
  1509.2 47.2 all-reduce.8
where the time goes:
time: 1600 us; the launch traced here: 1590 us
  waiting for transfers between devices  822 us (51%)
  blocking collectives  458 us (29%)
  local copies, waits for them, and re-layouts  104 us (6%)
  matrix products  94.5 us (6%)
  other arithmetic  68 us (4%)
  starting transfers between devices  28.6 us (2%)
    all_gather x4, waiting for transfers between devices, gather_rows(): return lax.all_gather(values, 'row', axis=0, tiled=True)  733 us
    all_gather x2, blocking collectives, back_to_middle(): full_weight = lax.all_gather(weight, 'row', axis=1, tiled=True)  126 us
    psum x4, blocking collectives, row_sum_values(): return lax.psum((pair[0], pair[1]), 'row')  105 us
    all_to_all x1, blocking collectives, local(): lax.all_to_all(cotangent, 'row', split_axis=2, concat_axis=0, tiled=True)  80.7 us
    all_gather x2, blocking collectives, project_in(): full_weight = lax.all_gather(weight, 'row', axis=0, tiled=True)  80.3 us
    all_to_all x1, blocking collectives, local(): lax.all_to_all(block_input, 'row', split_axis=2, concat_axis=0, tiled=True)  43.1 us
    all_gather x4, waiting for transfers between devices, gather_cols(): return lax.all_gather(values, 'col', axis=0, tiled=True)  36.2 us
  transfers between devices with their start and end apart: 19, of which 12 were waited for; matrix products, arithmetic and copies ran while one was open for 8% of the time, Pallas kernels for 0%

commit v1 on v0

v1 whole, which is shorter than its diff:
```python
import functools
import math

import jax
import jax.numpy as jnp
from jax import lax
from jax.experimental import pallas as pl
from jax.experimental.pallas import tpu as pltpu
from jax.sharding import PartitionSpec as P

EPS = 1e-06
ROOT_HALF = 0.7071067811865476
INV_ROOT_TWO_PI = 0.3989422804014327
LOG2E = 1.4426950408889634
F32, BF16 = jnp.float32, jnp.bfloat16


def mm(a, b, ca, cb):
    return lax.dot_general(a, b, (((ca,), (cb,)), ((), ())), preferred_element_type=F32)


def norm_parts(v):
    mean = jnp.mean(v, -1, keepdims=True)
    cen = v - mean
    rstd = lax.rsqrt(jnp.mean(cen * cen, -1, keepdims=True) + EPS)
    return cen * rstd, rstd


def norm_back(g, gain, xhat, rstd):
    gx = g * gain
    return rstd * (gx - jnp.mean(gx, -1, keepdims=True) - xhat * jnp.mean(gx * xhat, -1, keepdims=True))


def gelu_parts(u):
    cdf = 0.5 * (1.0 + lax.erf(u * ROOT_HALF))
    return u * cdf, cdf + u * jnp.exp(-0.5 * u * u) * INV_ROOT_TWO_PI


def kernel(cfg, x_hbm, c_hbm, wa, wup, wdn, g1, b1, qvb, ob, g2, b2, ub, db,
           y_out, dx_out, dg1, db1, dwa, dqvb, dob, dg2, db2, dup, dub, ddn, ddb,
           xin, cin, cb, xh1, a1, qkv, pt, o, h, xh2, rs1, rs2, a2, wot, bias3, gb, du, yacc, dacc,
           dhb, dout, dqkv, a1t, a2t, ct, dht, sems):
    NI, SEQ, SP, D, H, HD, FF, FC = cfg
    T = NI * SP
    E = HD
    cx = pltpu.make_async_copy(x_hbm, xin, sems.at[0])
    cc = pltpu.make_async_copy(c_hbm, cin, sems.at[1])
    cx.start()
    cc.start()
    xh1[:, SP - 16:, :] = jnp.zeros((NI, 16, D), F32)
    h[:, SP - 16:, :] = jnp.zeros((NI, 16, D), F32)
    yacc[:, SP - 16:, :] = jnp.zeros((NI, 16, D), F32)
    rs1[:, SP - 16:, :] = jnp.zeros((NI, 16, 1), F32)
    wot[...] = jnp.concatenate([wa[hh][:, 3 * E:] for hh in range(H)], axis=1)
    for hh in range(H):
        bias3[hh] = jnp.concatenate(
            [qvb[0:1, hh * E:(hh + 1) * E], jnp.zeros((1, E), F32),
             qvb[1:2, hh * E:(hh + 1) * E], jnp.zeros((1, E), F32)], axis=1)
    cx.wait()
    cc.wait()

    key_ok = lax.broadcasted_iota(jnp.int32, (SP, SP), 0) < SEQ

    def fwd(i, carry):
        xf = xin[i].astype(F32)
        xh, rstd = norm_parts(xf)
        xh1[i, :SEQ] = xh
        rs1[i, :SEQ] = rstd
        h[i, :SEQ] = xf
        yacc[i, :SEQ] = cin[i].astype(F32)
        cb[i] = yacc[i].astype(BF16)
        a = (xh1[i] * g1[...] + b1[...]).astype(BF16)
        a1[i] = a
        outs = []
        for hh in range(H):
            t = (mm(a, wa[hh], 1, 0) + bias3[hh]).astype(BF16)
            qkv[i, hh] = t
            q, k, v = t[:, :E], t[:, E:2 * E], t[:, 2 * E:3 * E]
            s = mm(k, q, 1, 1) * (LOG2E / math.sqrt(E))
            s = jnp.where(key_ok, s, -1e30)
            top = jnp.max(s, 0, keepdims=True)
            e = jnp.exp2(s - top)
            p = (e * (1.0 / jnp.sum(e, 0, keepdims=True))).astype(BF16)
            pt[i, hh] = p
            outs.append(mm(p, v, 0, 0).astype(BF16))
        oo = jnp.concatenate(outs, axis=1)
        o[i] = oo
        hh_ = h[i] + mm(oo, wot[...], 1, 1) + ob[...]
        h[i] = hh_
        xh, rstd = norm_parts(hh_)
        xh2[i] = xh
        rs2[i] = rstd
        a2[i] = (xh * g2[...] + b2[...]).astype(BF16)
        yacc[i] = hh_ + db[...]
        dacc[i] = jnp.zeros((SP, D), F32)
        return carry

    lax.fori_loop(0, NI, fwd, 0)
    a2t[...] = a2[...].reshape(T, D).T
    ct[...] = cb[...].reshape(T, D).T
    a1t[...] = a1[...].reshape(T, D).T

    NH = FF // wup.shape[2]
    FH = wup.shape[2]
    per = FH // FC

    def ff(f, carry):
        half, s = f // per, lax.rem(f, per)
        cols = pl.ds(pl.multiple_of(s * FC, FC), FC)
        w1, w2 = wup[half, :, cols], wdn[half, :, cols]
        bias = ub[pl.ds(half, 1), cols]

        def one(i, tot):
            u = mm(a2[i], w1, 1, 0) + bias
            act, slope = gelu_parts(u)
            gbi = act.astype(BF16)
            d = mm(cb[i], w2, 1, 0) * slope
            dui = d.astype(BF16)
            gb[i] = gbi
            du[i] = dui
            yacc[i] += mm(gbi, w2, 1, 1)
            dacc[i] += mm(dui, w1, 1, 1)
            return tot + jnp.sum(d, 0, keepdims=True)

        tot = lax.fori_loop(0, NI, one, jnp.zeros((1, FC), F32))
        dub[pl.ds(half, 1), cols] = tot
        ddn[half, :, cols] = mm(ct[...], gb[...].reshape(T, FC), 1, 0)
        dup[half, :, cols] = mm(a2t[...], du[...].reshape(T, FC), 1, 0)
        return carry

    lax.fori_loop(0, NH * per, ff, 0)

    def mid(i, carry):
        s_db, s_g, s_b, s_ob = carry
        y_out[i] = yacc[i][:SEQ].astype(BF16)
        c = cb[i].astype(F32)
        da = dacc[i]
        xh = xh2[i]
        dh = c + norm_back(da, g2[...], xh, rs2[i])
        h[i] = dh
        db_ = dh.astype(BF16)
        dhb[i] = db_
        dd = mm(db_, wot[...], 1, 0).astype(BF16)
        for hh in range(H):
            dout[i, hh] = dd[:, hh * E:(hh + 1) * E]
        dacc[i] = jnp.zeros((SP, D), F32)
        add = lambda t, v: t + jnp.sum(v, 0, keepdims=True)
        return add(s_db, c), add(s_g, da * xh), add(s_b, da), add(s_ob, dh)

    z = jnp.zeros((1, D), F32)
    s_db, s_g, s_b, s_ob = lax.fori_loop(0, NI, mid, (z, z, z, z))
    ddb[...] = s_db
    dg2[...] = s_g
    db2[...] = s_b
    dob[...] = s_ob
    dht[...] = dhb[...].reshape(T, D).T
    dwo = mm(dht[...], o[...].reshape(T, D), 1, 0)

    scale = 1.0 / math.sqrt(E)

    def back(hh, carry):
        def one(i, tot):
            t = qkv[i, hh]
            q, k, v = t[:, :E], t[:, E:2 * E], t[:, 2 * E:3 * E]
            p = pt[i, hh]
            do = dout[i, hh]
            pf = p.astype(F32)
            dp = mm(v, do, 1, 1)
            delta = jnp.sum(pf * dp, 0, keepdims=True)
            ds = (pf * (dp - delta)).astype(BF16)
            dk = mm(ds, q, 1, 0) * scale
            dv = mm(p, do, 1, 0)
            dq = mm(ds, k, 0, 0) * scale
            dd = jnp.concatenate([dq, dk, dv, jnp.zeros((SP, E), F32)], axis=1)
            db_ = dd.astype(BF16)
            dqkv[i] = db_
            dacc[i] += mm(db_, wa[hh], 1, 1)
            return tot + jnp.sum(dd, 0, keepdims=True)

        tot = lax.fori_loop(0, NI, one, jnp.zeros((1, 4 * E), F32))
        dqvb[hh] = tot
        dwa[hh] = mm(a1t[...], dqkv[...].reshape(T, 4 * E), 1, 0)
        return carry

    lax.fori_loop(0, H, back, 0)
    for hh in range(H):
        dwa[hh, :, 3 * E:] = dwo[:, hh * E:(hh + 1) * E]

    def last(i, carry):
        s_g, s_b = carry
        da = dacc[i]
        xh = xh1[i]
        dx = h[i] + norm_back(da, g1[...], xh, rs1[i])
        dx_out[i] = dx[:SEQ]
        add = lambda t, v: t + jnp.sum(v, 0, keepdims=True)
        return add(s_g, da * xh), add(s_b, da)

    s_g, s_b = lax.fori_loop(0, NI, last, (z, z))
    dg1[...] = s_g
    db1[...] = s_b


def compute(x, c, wa, wup, wdn, g1, b1, qvb, ob, g2, b2, ub, db, fc=768):
    NI, SEQ, D = x.shape
    H, _, W4 = wa.shape
    HD = W4 // 4
    C, _, FH = wup.shape
    FF = C * FH
    SP = -(-SEQ // 16) * 16
    T = NI * SP
    cfg = (NI, SEQ, SP, D, H, HD, FF, fc)
    V = pl.BlockSpec(memory_space=pltpu.VMEM)
    A = pl.BlockSpec(memory_space=pl.ANY)
    sd = jax.ShapeDtypeStruct
    vm = pltpu.VMEM
    return pl.pallas_call(
        functools.partial(kernel, cfg),
        out_shape=(sd((NI, SEQ, D), BF16), sd((NI, SEQ, D), F32), sd((1, D), F32), sd((1, D), F32),
                   sd((H, D, W4), F32), sd((H, 1, W4), F32), sd((1, D), F32), sd((1, D), F32), sd((1, D), F32),
                   sd((C, D, FH), F32), sd((C, FH), F32), sd((C, D, FH), F32), sd((1, D), F32)),
        in_specs=[A, A] + [V] * 11,
        out_specs=[V] * 13,
        scratch_shapes=[
            vm((NI, SEQ, D), BF16), vm((NI, SEQ, D), BF16), vm((NI, SP, D), BF16), vm((NI, SP, D), F32),
            vm((NI, SP, D), BF16), vm((NI, H, SP, 4 * HD), BF16), vm((NI, H, SP, SP), BF16), vm((NI, SP, D), BF16),
            vm((NI, SP, D), F32), vm((NI, SP, D), F32), vm((NI, SP, 1), F32), vm((NI, SP, 1), F32),
            vm((NI, SP, D), BF16), vm((D, D), BF16), vm((H, 1, 4 * HD), F32), vm((NI, SP, fc), BF16), vm((NI, SP, fc), BF16),
            vm((NI, SP, D), F32), vm((NI, SP, D), F32), vm((NI, SP, D), BF16), vm((NI, H, SP, HD), BF16),
            vm((NI, SP, 4 * HD), BF16), vm((D, T), BF16), vm((D, T), BF16), vm((D, T), BF16), vm((D, T), BF16),
            pltpu.SemaphoreType.DMA((2,)),
        ],
        compiler_params=pltpu.CompilerParams(vmem_limit_bytes=67043328),
    )(x, c, wa, wup, wdn, g1, b1, qvb, ob, g2, b2, ub, db)


def local(x, g1, b1, aw, qvb, ob, g2, b2, up, ub, dn, db, c):
    gr = lambda v, ax: lax.all_gather(v, "row", axis=ax, tiled=True)
    vec = jnp.stack([g1, b1, ob, g2, b2, db])
    vec = gr(vec, 1)
    g1, b1, ob, g2, b2, db = [vec[i:i + 1] for i in range(6)]
    rows = aw.shape[1]
    wa = lax.all_gather(gr(aw, 1), "col", axis=0, tiled=True)
    wup = lax.all_gather(gr(up, 0), "col", axis=0)
    wdn = lax.all_gather(gr(dn, 0), "col", axis=0)
    qvb_ = lax.all_gather(qvb, "col", axis=1, tiled=True)
    ub_ = lax.all_gather(ub, "col", axis=0)
    y, dx, dg1, db1, dwa, dqvb, dob, dg2, db2, dup, dub, ddn, ddb = compute(
        x, c, wa, wup, wdn, g1, b1, qvb_, ob, g2, b2, ub_, db, fc=up.shape[1])

    def scatter(g, cdim, rdim):
        g = g.astype(BF16)
        g = lax.psum_scatter(g, "row", scatter_dimension=rdim, tiled=True)
        g = lax.psum_scatter(g, "col", scatter_dimension=cdim, tiled=True)
        return lax.psum(g, "dp").astype(F32)

    dwa = scatter(dwa, 0, 1)
    dup = scatter(dup, 0, 1)[0]
    ddn = scatter(ddn, 0, 1)[0]
    hd = aw.shape[2] // 4
    small = lax.psum(jnp.concatenate([dg1[0], db1[0], dob[0], dg2[0], db2[0], ddb[0], dqvb[:, 0, :hd].reshape(-1),
                                      dqvb[:, 0, 2 * hd:3 * hd].reshape(-1), dub.reshape(-1)]), ("dp", "row", "col"))
    d = g1.shape[1]
    r, k = lax.axis_index("row"), lax.axis_index("col")
    rp = [lax.dynamic_slice(small, (i * d + r * rows,), (rows,)) for i in range(6)]
    qc = qvb.shape[1]
    dq = [lax.dynamic_slice(small, ((6 + i) * d + k * qc,), (qc,)) for i in range(2)]
    du = lax.dynamic_slice(small, (8 * d + k * ub.shape[0],), (ub.shape[0],))
    return y, dx, rp[0], rp[1], dwa, jnp.stack(dq), rp[2], rp[3], rp[4], dup, du, ddn, rp[5]


def solution(mesh):
    placed = (
        P(("dp", "row", "col"), None, None),
        P("row"),
        P("row"),
        P("col", "row", None),
        P(None, "col"),
        P("row"),
        P("row"),
        P("row"),
        P("row", "col"),
        P("col"),
        P("row", "col"),
        P("row"),
        P(("dp", "row", "col"), None, None),
    )
    return jax.shard_map(
        local,
        mesh=mesh,
        in_specs=placed,
        out_specs=(
            P(("dp", "row", "col"), None, None),
            P(("dp", "row", "col"), None, None),
            P("row"),
            P("row"),
            P("col", "row", None),
            P(None, "col"),
            P("row"),
            P("row"),
            P("row"),
            P("row", "col"),
            P("col"),
            P("row", "col"),
            P("row"),
        ),
        check_vma=False,
    )
```

time: 1600 us -> 338 us (0.21)
  waiting for transfers between devices: 822 us -> 124 us
  blocking collectives: 458 us -> 111 us
  local copies, waits for them, and re-layouts: 104 us -> 3.67 us
  matrix products: 94.5 us -> 0 us
  Pallas kernels: 0 us -> 72.5 us
  other arithmetic: 68 us -> 12.6 us
  starting transfers between devices: 28.6 us -> 0.4 us
    all_gather x8 -> x3, waiting for transfers between devices: 769 us -> 0.02 us  [the longest x1 0.01 us: local(): wdn = lax.all_gather(gr(dn, 0), 'col', axis=0)]
    all_gather x4 -> x6, blocking collectives: 207 us -> 69.9 us  [the longest x4 66.3 us: local(): gr = lambda v, ax: lax.all_gather(v, 'row', axis=ax, tiled=True)]
    all_to_all x2 -> x0, blocking collectives: 124 us -> none  [the longest x1 80.7 us: local(): lax.all_to_all(cotangent, 'row', split_axis=2, concat_axis=0, tiled=True)]
    reduce_scatter x4 -> x6, waiting for transfers between devices: 21.8 us -> 117 us  [the longest x3 86.2 us: scatter(): g = lax.psum_scatter(g, 'row', scatter_dimension=rdim, tiled=True)]
    dot_general x26 -> x0, matrix products: 94.5 us -> none  [the longest x4 28 us: token_product(): lax.dot_general(left, incoming_gradient, (((0, 1), (0, 1)), ((), ())), pr...]
    psum x6 -> x1, blocking collectives: 127 us -> 40.7 us  [local(): lax.psum(jnp.concatenate([dg1[0], db1[0], dob[0], dg2[0], db2[0], ddb[0],...]
    pallas_call x0 -> x1, Pallas kernels: none -> 72.5 us  [compute(): pl.pallas_call(functools.partial(kernel, cfg), out_shape=(sd((NI, SEQ, D)...]
    all_to_all x13 -> x0, local copies, waits for them, and re-layouts: 51.8 us -> none  [the longest x4 21.6 us: back_to_middle(): lax.all_to_all(whole_grad, 'row', split_axis=0, concat_axis=2, tiled=True)]
  transfers between devices with their start and end apart: 19 -> 10, of which waited for: 12 -> 7; matrix products, arithmetic and copies ran while one was open for 8% -> 2% of each run, Pallas kernels for 0% -> 0%
where the time goes in v1:
time: 338 us
  waiting for transfers between devices  124 us (37%)
  blocking collectives  111 us (33%)
  Pallas kernels  72.5 us (21%)
  between operations  14.5 us (4%)
  other arithmetic  12.6 us (4%)
  local copies, waits for them, and re-layouts  3.67 us (1%)
    reduce_scatter x3, waiting for transfers between devices, scatter(): g = lax.psum_scatter(g, 'row', scatter_dimension=rdim, tiled=True)  86.2 us
    pallas_call x1, Pallas kernels, compute(): pl.pallas_call(functools.partial(kernel, cfg), out_shape=(sd((NI, SEQ, D)...  72.5 us
    all_gather x4, blocking collectives, local(): gr = lambda v, ax: lax.all_gather(v, 'row', axis=ax, tiled=True)  66.3 us
    psum x1, blocking collectives, local(): lax.psum(jnp.concatenate([dg1[0], db1[0], dob[0], dg2[0], db2[0], ddb[0],...  40.7 us
    reduce_scatter x3, waiting for transfers between devices, scatter(): g = lax.psum_scatter(g, 'col', scatter_dimension=cdim, tiled=True)  30.5 us
    convert_element_type x3, other arithmetic, scatter(): g = g.astype(BF16)  6.96 us
    psum x1, waiting for transfers between devices, scatter(): return lax.psum(g, 'dp').astype(F32)  6.82 us
  transfers between devices with their start and end apart: 10, of which 7 were waited for; matrix products, arithmetic and copies ran while one was open for 2% of the time, Pallas kernels for 0%

profile of v1, /device:TPU:0, one launch (start us, length us, event | category | flops | bytes accessed | tf_op | source)
XLA Modules:
  0.0 338.0 jit_solution(17500375905201905123)
XLA Ops:
  7.2 20.2 %all_gather.36 = bf16[3,384,256]{2,1,0:T(8,128)(2,1)} all-gather(bf16[3,96,256]{2,1,0:T(8,128)(2,1)} %param.16), channel_id=1, replica_groups=mesh['dp'=4,'row'=4,'col'=2] {'row'}, dimensions={1}, use_global_device_ids=true | all-gather | bytes 737280 | tf_op jit(solution)/shard_map/all_gather | solution.py:237
  27.6 16.3 %all_gather.38 = bf16[384,768]{1,0:T(8,128)(2,1)} all-gather(bf16[96,768]{1,0:T(8,128)(2,1)S(1)} %copy-done.1), channel_id=1, replica_groups=mesh['dp'=4,'row'=4,'col'=2] {'row'}, dimensions={0}, use_global_device_ids=true | all-gather | bytes 737280 | tf_op jit(solution)/shard_map/all_gather | solution.py:237
  44.0 16.5 %all_gather.41 = bf16[384,768]{1,0:T(8,128)(2,1)} all-gather(bf16[96,768]{1,0:T(8,128)(2,1)S(1)} %copy-done.2), channel_id=1, replica_groups=mesh['dp'=4,'row'=4,'col'=2] {'row'}, dimensions={0}, use_global_device_ids=true | all-gather | bytes 737280 | tf_op jit(solution)/shard_map/all_gather | solution.py:237
  60.7 13.2 %all-gather.3 = f32[4,96,6]{1,2,0:T(8,128)S(1)} all-gather(f32[1,96,6]{1,2,0:T(8,128)S(1)} %bitcast.33), channel_id=1, replica_groups=mesh['dp'=4,'row'=4,'col'=2] {'row'}, dimensions={0}, use_global_device_ids=true | all-gather | bytes 11520 | tf_op jit(solution)/shard_map/all_gather | solution.py:237
  74.0 1.8 all-gather.5
  76.5 1.8 all-gather.4
  78.3 0.7 reshape.36
  79.0 0.6 fusion.2
  79.6 72.5 %shard_map.228 = (bf16[6,197,384]{2,1,0:T(8,128)(2,1)}, f32[6,197,384]{2,1,0:T(8,128)}, f32[1,384]{1,0:T(1,128)}, f32[1,384]{1,0:T(1,128)}, f32[6,384,256]{2,1,0...) custom-call(bf16[6,197,384]{2,1,0:T(8,128)(2,1)} %x_hbm.1, ...), custom_call_target="tpu_custom_call" | custom-call | tf_op jit(solution)/shard_map/pallas_call | solution.py:216
  152.1 2.8 convert_element_type.16
  154.9 3.0 convert_element_type.17
  158.0 1.2 convert_element_type.14
  159.3 26.3 %reduce-scatter.11.cloned.1.call-done = bf16[2,96,768]{2,1,0:T(8,128)(2,1)} async-done(((bf16[2,384,768]{2,1,0:T(8,128)(2,1)}), bf16[2,96,768]{2,1,0:T(8,128)(2,1)}) %reduce-scatter.11.cloned.1.call-update) | async-done | bytes 294928 | tf_op jit(solution)/shard_map/reduce_scatter | solution.py:252
  185.7 30.0 %reduce-scatter.15.cloned.1.call-done = bf16[2,96,768]{2,1,0:T(8,128)(2,1)} async-done(((bf16[2,384,768]{2,1,0:T(8,128)(2,1)}), bf16[2,96,768]{2,1,0:T(8,128)(2,1)}) %reduce-scatter.15.cloned.1.call-update) | async-done | bytes 294928 | tf_op jit(solution)/shard_map/reduce_scatter | solution.py:252
  216.0 29.9 %reduce-scatter.7.cloned.1.call-done = bf16[6,96,256]{2,1,0:T(8,128)(2,1)} async-done(((bf16[6,384,256]{2,1,0:T(8,128)(2,1)}), bf16[6,96,256]{2,1,0:T(8,128)(2,1)}) %reduce-scatter.7.cloned.1.call-update) | async-done | bytes 294928 | tf_op jit(solution)/shard_map/reduce_scatter | solution.py:252
  246.3 8.2 %reduce-scatter.13.cloned.1.call-done = bf16[1,96,768]{2,1,0:T(8,128)(2,1)} async-done(((bf16[2,96,768]{2,1,0:T(8,128)(2,1)}), bf16[1,96,768]{2,1,0:T(8,128)(2,1)}) %reduce-scatter.13.cloned.1.call-update) | async-done | bytes 147472 | tf_op jit(solution)/shard_map/reduce_scatter | solution.py:253
  254.5 11.1 %reduce-scatter.17.cloned.1.call-done = bf16[1,96,768]{2,1,0:T(8,128)(2,1)} async-done(((bf16[2,96,768]{2,1,0:T(8,128)(2,1)}), bf16[1,96,768]{2,1,0:T(8,128)(2,1)}) %reduce-scatter.17.cloned.1.call-update) | async-done | bytes 147472 | tf_op jit(solution)/shard_map/reduce_scatter | solution.py:253
  265.6 11.1 %reduce-scatter.9.cloned.1.call-done = bf16[3,96,256]{2,1,0:T(8,128)(2,1)} async-done(((bf16[6,96,256]{2,1,0:T(8,128)(2,1)}), bf16[3,96,256]{2,1,0:T(8,128)(2,1)}) %reduce-scatter.9.cloned.1.call-update) | async-done | bytes 147472 | tf_op jit(solution)/shard_map/reduce_scatter | solution.py:253
  276.8 40.7 %psum.28 = f32[4608]{0:T(1024)S(1)} all-reduce(f32[4608]{0:T(1024)S(1)} %constant_dynamic-update-slice_fusion), channel_id=1, replica_groups=mesh['dp'=4,'row'=4,'col'=2] {'dp','row','col'}, use_global_device_ids=true, to_apply=%region_0.0 | all-reduce | flops 4608 | bytes 36864 | tf_op jit(solution)/shard_map/psum | solution.py:260
  317.5 0.7 dynamic_slice.34
  319.4 6.8 %all-reduce.3.cloned.1.call-done = (bf16[3,96,256]{2,1,0:T(8,128)(2,1)}, bf16[96,768]{1,0:T(8,128)(2,1)}, bf16[96,768]{1,0:T(8,128)(2,1)}) async-done(((bf16[3,96,256]{2,1,0:T(8,128)(2,1)}, bf16[96,768]{1,0:T(8,128)(2,1)}, bf16[96,768]{1,0:T(8,128)(2,1)}), (bf16[3,96,256]{2,1,0:T(8,128)(2,1)}, bf16[96,768]{1,0:T(8,128)(2,1)}, bf16[96,768]{1,0:T(8,128)(2,1)})) %all-reduce.3.cloned.1.call-update) | async-done | bytes 442384 | tf_op jit(solution)/shard_map/psum | solution.py:254
  326.3 1.6 convert_element_type.15
  327.9 1.6 squeeze.37
  329.5 1.6 squeeze.39
  (90 shorter events, 3.0 us)
Async XLA Ops:
  7.2 36.8 %copy-start.2 = (bf16[96,768]{1,0:T(8,128)(2,1)S(1)}, bf16[96,768]{1,0:T(8,128)(2,1)}, u32[]{:S(2)}) copy-start(bf16[96,768]{1,0:T(8,128)(2,1)} %param.23) | copy-start | bytes 442372
  7.2 72.4 %all-gather.10.cloned.1.call-start = ((), (), s32[]{:S(2)}) async-start(), calls=%async_computation.6 | async-start | bytes 1769472 | tf_op jit(solution)/shard_map/all_gather | solution.py:242
  27.5 33.1 %copy-start.13 = (f32[96]{0:T(128)S(1)}, f32[96]{0:T(128)}, u32[]{:S(2)}) copy-start(f32[96]{0:T(128)} %param.14) | copy-start | bytes 1156
  27.5 33.1 %copy-start.14 = (f32[96]{0:T(128)S(1)}, f32[96]{0:T(128)}, u32[]{:S(2)}) copy-start(f32[96]{0:T(128)} %param.15) | copy-start | bytes 1156
  27.5 33.1 %copy-start.15 = (f32[96]{0:T(128)S(1)}, f32[96]{0:T(128)}, u32[]{:S(2)}) copy-start(f32[96]{0:T(128)} %param.18) | copy-start | bytes 1156
  27.5 33.1 %copy-start.16 = (f32[96]{0:T(128)S(1)}, f32[96]{0:T(128)}, u32[]{:S(2)}) copy-start(f32[96]{0:T(128)} %param.19) | copy-start | bytes 1156
  27.6 33.1 %copy-start.17 = (f32[96]{0:T(128)S(1)}, f32[96]{0:T(128)}, u32[]{:S(2)}) copy-start(f32[96]{0:T(128)} %param.20) | copy-start | bytes 1156
  27.6 52.0 %all-gather.12.cloned.1.call-start = ((), (), s32[]{:S(2)}) async-start(), calls=%async_computation.13 | async-start | bytes 1769472 | tf_op jit(solution)/shard_map/all_gather | solution.py:243
  44.0 35.6 %all-gather.14.cloned.1.call-start = ((), (), s32[]{:S(2)}) async-start(), calls=%async_computation.14 | async-start | bytes 1769472 | tf_op jit(solution)/shard_map/all_gather | solution.py:244
  60.6 125.0 %reduce-scatter.11.cloned.1.call-start = ((), (), s32[]{:S(2)}) async-start(), calls=%async_computation.9 | async-start | bytes 1474560 | tf_op jit(solution)/shard_map/reduce_scatter | solution.py:252
  154.9 60.8 %reduce-scatter.15.cloned.1.call-start = ((), (), s32[]{:S(2)}) async-start(), calls=%async_computation.11 | async-start | bytes 1474560 | tf_op jit(solution)/shard_map/reduce_scatter | solution.py:252
  158.0 87.9 %reduce-scatter.7.cloned.1.call-start = ((), (), s32[]{:S(2)}) async-start(), calls=%async_computation.7 | async-start | bytes 1474560 | tf_op jit(solution)/shard_map/reduce_scatter | solution.py:252
  159.2 56.6 %copy-start.12 = (f32[1,384]{1,0:T(1,128)S(1)}, f32[1,384]{1,0:T(1,128)}, u32[]{:S(2)}) copy-start(f32[1,384]{1,0:T(1,128)} %get-tuple-element.28) | copy-start | bytes 4612
  159.2 56.7 %copy-start.11 = (f32[1,384]{1,0:T(1,128)S(1)}, f32[1,384]{1,0:T(1,128)}, u32[]{:S(2)}) copy-start(f32[1,384]{1,0:T(1,128)} %get-tuple-element.29) | copy-start | bytes 4612
  159.2 56.7 %copy-start.10 = (f32[1,384]{1,0:T(1,128)S(1)}, f32[1,384]{1,0:T(1,128)}, u32[]{:S(2)}) copy-start(f32[1,384]{1,0:T(1,128)} %get-tuple-element.30) | copy-start | bytes 4612
  159.2 56.7 %copy-start.4 = (f32[6,1,256]{2,1,0:T(1,128)S(1)}, f32[6,1,256]{2,1,0:T(1,128)}, u32[]{:S(2)}) copy-start(f32[6,1,256]{2,1,0:T(1,128)} %get-tuple-element.34) | copy-start | bytes 18436
  159.2 86.7 %copy-start.9 = (f32[1,384]{1,0:T(1,128)S(1)}, f32[1,384]{1,0:T(1,128)}, u32[]{:S(2)}) copy-start(f32[1,384]{1,0:T(1,128)} %get-tuple-element.31) | copy-start | bytes 4612
  159.2 86.8 %copy-start.8 = (f32[1,384]{1,0:T(1,128)S(1)}, f32[1,384]{1,0:T(1,128)}, u32[]{:S(2)}) copy-start(f32[1,384]{1,0:T(1,128)} %get-tuple-element.32) | copy-start | bytes 4612
  159.2 86.8 %copy-start.7 = (f32[1,384]{1,0:T(1,128)S(1)}, f32[1,384]{1,0:T(1,128)}, u32[]{:S(2)}) copy-start(f32[1,384]{1,0:T(1,128)} %get-tuple-element.33) | copy-start | bytes 4612
  159.2 86.9 %copy-start.3 = (f32[2,768]{1,0:T(2,128)S(1)}, f32[2,768]{1,0:T(2,128)}, u32[]{:S(2)}) copy-start(f32[2,768]{1,0:T(2,128)} %get-tuple-element.35) | copy-start | bytes 18436
  159.3 95.2 %reduce-scatter.13.cloned.1.call-start = ((), (), s32[]{:S(2)}) async-start(), calls=%async_computation.10 | async-start | bytes 442368 | tf_op jit(solution)/shard_map/reduce_scatter | solution.py:253
  185.7 80.0 %reduce-scatter.17.cloned.1.call-start = ((), (), s32[]{:S(2)}) async-start(), calls=%async_computation.12 | async-start | bytes 442368 | tf_op jit(solution)/shard_map/reduce_scatter | solution.py:253
  215.7 61.0 %reduce-scatter.9.cloned.1.call-start = ((), (), s32[]{:S(2)}) async-start(), calls=%async_computation.8 | async-start | bytes 442368 | tf_op jit(solution)/shard_map/reduce_scatter | solution.py:253
  245.9 80.4 %all-reduce.3.cloned.1.call-start = ((), (), s32[]{:S(2)}) async-start(), calls=%async_computation.15 | async-start | bytes 884736 | tf_op jit(solution)/shard_map/psum | solution.py:254
  (5 other events, 119.3 us)
Sparse Core Ops, SparseCore 0:
  27.6 8.9 all-gather.9
  44.1 9.5 all-gather.11
  60.7 10.4 all-gather.13
  155.0 30.5 reduce-scatter.10
  187.8 27.8 reduce-scatter.14
  217.9 27.9 reduce-scatter.6
  248.1 6.3 reduce-scatter.12
  256.7 8.8 reduce-scatter.16
  267.8 8.8 reduce-scatter.8
  279.9 46.3 all-reduce.2

commit v2 on v1

v2 whole, which is shorter than its diff:
```python
import functools
import math

import jax
import jax.numpy as jnp
from jax import lax
from jax.experimental import pallas as pl
from jax.experimental.pallas import tpu as pltpu
from jax.sharding import PartitionSpec as P

EPS = 1e-06
ROOT_HALF = 0.7071067811865476
INV_ROOT_TWO_PI = 0.3989422804014327
LOG2E = 1.4426950408889634
F32, BF16 = jnp.float32, jnp.bfloat16
MESH = pl.DeviceIdType.MESH


def mm(a, b, ca, cb):
    return lax.dot_general(a, b, (((ca,), (cb,)), ((), ())), preferred_element_type=F32)


def norm_parts(v):
    mean = jnp.mean(v, -1, keepdims=True)
    cen = v - mean
    rstd = lax.rsqrt(jnp.mean(cen * cen, -1, keepdims=True) + EPS)
    return cen * rstd, rstd


def norm_back(g, gain, xhat, rstd):
    gx = g * gain
    return rstd * (gx - jnp.mean(gx, -1, keepdims=True) - xhat * jnp.mean(gx * xhat, -1, keepdims=True))


def gelu_parts(u):
    w = u * ROOT_HALF
    cdf = 0.5 + 0.5 * lax.erf(w)
    bell = jnp.exp2((w * w) * -LOG2E)
    return u * cdf, cdf + (w * bell) * (INV_ROOT_TWO_PI / ROOT_HALF)


def rsum(v):
    return jnp.sum(v, 0, keepdims=True)


class Shift:
    def __init__(self, axis, n):
        self.axis, self.n, self.me = axis, n, lax.axis_index(axis)

    def up(self, k):
        return lax.rem(self.me + k, self.n)

    def down(self, k):
        return lax.rem(self.me + self.n - k, self.n)

    def ks(self):
        return range(1, self.n)


def remote(src, dst, ssem, rsem, axis, to):
    return pltpu.make_async_remote_copy(
        src_ref=src, dst_ref=dst, send_sem=ssem, recv_sem=rsem, device_id={axis: to}, device_id_type=MESH)


class Reduce:
    def __init__(self, cfg, ax, bufs, sems):
        self.rows, self.split = cfg
        self.dp, self.row, self.col = ax
        (self.send_c, self.recv_c, self.send_p, self.recv_p, self.send_z, self.recv_z, self.fin) = bufs
        self.sems = sems
        self.np = self.send_p.shape[0]
        self.c, self.p, self.z, self.a = [], [], [], []

    def put_c(self, k, a, v):
        self.send_c[k - 1, a] = v.astype(BF16)

    def start_c(self, k):
        self.c.append(remote(self.send_c.at[k - 1], self.recv_c.at[k - 1], self.sems.at[0, k], self.sems.at[1, k],
                             self.col.axis, self.col.up(k)))
        self.c[-1].start()

    def wait_c(self):
        for cp in self.c:
            cp.wait_recv()

    def put_p(self, a, v):
        sr, sl = self.split
        pr, pl_ = self.send_p.shape[-2:]
        for k in self.col.ks():
            v = v + self.recv_c[k - 1, a].astype(F32)
        for r in range(self.row.n):
            for qr in range(sr):
                for ql in range(sl):
                    lo = r * self.rows + qr * pr
                    piece = v[lo:lo + pr, ql * pl_:(ql + 1) * pl_].astype(BF16)
                    self.send_p[qr * sl + ql, r, a] = piece
                    if self.np == 1:
                        self.recv_p[self.dp.me, r, a] = piece

    def start_p(self):
        for k in self.dp.ks():
            to = self.dp.up(k)
            self.p.append(remote(self.send_p.at[to if self.np > 1 else 0], self.recv_p.at[self.dp.me],
                                 self.sems.at[2, k], self.sems.at[3, k], self.dp.axis, to))
            self.p[-1].start()

    def start_z(self):
        for cp in self.p:
            cp.wait_recv()
        if self.np > 1:
            t = self.send_p[self.dp.me].astype(F32)
            for k in self.dp.ks():
                t = t + self.recv_p[self.dp.up(k)].astype(F32)
        else:
            t = self.recv_p[0].astype(F32)
            for q in range(1, self.dp.n):
                t = t + self.recv_p[q].astype(F32)
        self.send_z[...] = t.astype(BF16)
        for k in self.row.ks():
            to = self.row.up(k)
            self.z.append(remote(self.send_z.at[to], self.recv_z.at[self.row.me], self.sems.at[4, k], self.sems.at[5, k],
                                 self.row.axis, to))
            self.z[-1].start()

    def start_a(self):
        for cp in self.z:
            cp.wait_recv()
        t = self.send_z[self.row.me].astype(F32)
        for k in self.row.ks():
            t = t + self.recv_z[self.row.up(k)].astype(F32)
        me = self.dp.me if self.np > 1 else 0
        self.fin[me] = t.astype(BF16)
        if self.np > 1:
            for k in self.dp.ks():
                self.a.append(remote(self.fin.at[me], self.fin.at[me], self.sems.at[6, k], self.sems.at[7, k],
                                     self.dp.axis, self.dp.up(k)))
                self.a[-1].start()

    def finish(self, put):
        sr, sl = self.split
        pr, pl_ = self.send_p.shape[-2:]
        for cp in self.a:
            cp.wait_recv()
        for a in range(self.fin.shape[1]):
            for qr in range(sr):
                for ql in range(sl):
                    put(a, slice(qr * pr, (qr + 1) * pr), slice(ql * pl_, (ql + 1) * pl_),
                        self.fin[qr * sl + ql, a].astype(F32))
        for cp in self.c + self.p + self.z + self.a:
            cp.wait_send()


def kernel(cfg, *refs):
    (DP, R, C, NI, SEQ, SP, D, Hc, E, FH, rows, split) = cfg
    (x_hbm, g1_h, b1_h, aw_h, qvb_h, ob_h, g2_h, b2_h, up_h, ub_h, dn_h, db_h, c_hbm) = refs[:13]
    (y_o, dx_o, dg1_o, db1_o, daw_o, dqvb_o, dob_o, dg2_o, db2_o, dup_o, dub_o, ddn_o, ddb_o) = refs[13:26]
    (wa, wup, wdn, vall, qvall, uball, vec, bias3, xin, cin, cb, xh1, rs1, a1, qkv, pt, o, h, xh2, rs2, a2, wot, gb, du,
     yacc, dacc, dout, dqkv, a2t, ct, dwo, dxb, dubs, dqvs,
     f1, f2, f3, f4, f5, f6, f7, t1, t2, t3, t4, t5, t6, t7, so_f, so_t,
     sgs, sgc, sgp, sgz, sgr,
     lsem, osem, wz, wp, wc, fsem, tsem, vsem, gsem) = refs[26:]
    H, T, W4 = C * Hc, NI * SP, 4 * E
    dp, row, col = Shift("dp", DP), Shift("row", R), Shift("col", C)
    d, r, c = dp.me, row.me, col.me
    sr, sl = split
    np_ = sr * sl
    part = np_ > 1

    loads = [pltpu.make_async_copy(x_hbm, xin, lsem.at[0]), pltpu.make_async_copy(c_hbm, cin, lsem.at[1])]
    own = pl.ds(pl.multiple_of(r * rows, rows), rows)
    heads = pl.ds(c * Hc, Hc)
    wloads = [pltpu.make_async_copy(aw_h, wa.at[heads, own, :], lsem.at[10]),
              pltpu.make_async_copy(up_h, wup.at[c, own, :], lsem.at[11]),
              pltpu.make_async_copy(dn_h, wdn.at[c, own, :], lsem.at[12])]
    for cp in loads + wloads:
        cp.start()
    for i, v in enumerate([g1_h, b1_h, ob_h, g2_h, b2_h, db_h]):
        vall[r, i:i + 1, 0:rows] = v[...].reshape(1, rows)
    qvall[c] = qvb_h[...]
    uball[c] = ub_h[...].reshape(1, FH)

    barrier = pltpu.get_barrier_semaphore()
    for ax in (dp, row, col):
        for k in ax.ks():
            pl.semaphore_signal(barrier, inc=1, device_id={ax.axis: ax.up(k)}, device_id_type=MESH)

    xh1[:, SP - 16:, :] = jnp.zeros((NI, 16, D), F32)
    h[:, SP - 16:, :] = jnp.zeros((NI, 16, D), F32)
    yacc[:, SP - 16:, :] = jnp.zeros((NI, 16, D), F32)
    rs1[:, SP - 16:, :] = jnp.zeros((NI, 16, 1), F32)
    sgs[...] = jnp.zeros(sgs.shape, F32)
    loads[0].wait()

    def norm1(i, carry):
        xf = xin[i].astype(F32)
        xh, rstd = norm_parts(xf)
        xh1[i, :SEQ] = xh
        rs1[i, :SEQ] = rstd
        h[i, :SEQ] = xf
        return carry

    lax.fori_loop(0, NI, norm1, 0)
    pl.semaphore_wait(barrier, (DP - 1) + (R - 1) + (C - 1))

    def block(ref, hh, rr, q):
        pr, pw = rows // sr, ref.shape[2] // sl
        return ref.at[hh, pl.ds(pl.multiple_of(rr * rows + (q // sl) * pr, pr), pr),
                      pl.ds(pl.multiple_of(lax.rem(q, sl) * pw, pw), pw)]

    def shard(ref, q):
        pr, pw = rows // sr, ref.shape[-1] // sl
        cut = (pl.ds(pl.multiple_of((q // sl) * pr, pr), pr), pl.ds(pl.multiple_of(lax.rem(q, sl) * pw, pw), pw))
        return ref.at[(slice(None),) + cut] if len(ref.shape) == 3 else ref.at[cut]

    piece = d if part else 0
    weights = [(aw_h, wa, heads), (up_h, wup, c), (dn_h, wdn, c)]

    def gather_z(i):
        src, dst, hh = weights[i]
        out = []
        for k in row.ks():
            out.append(remote(shard(src, piece), block(dst, hh, r, piece), wz.at[0, i, k], wz.at[1, i, k], "row", row.up(k)))
            out[-1].start()
        return out

    def gather_p(i, zs):
        _, dst, hh = weights[i]
        out = []
        for cp, k in zip(zs, row.ks()):
            cp.wait_recv()
            if part:
                for kd in dp.ks():
                    b = block(dst, hh, row.down(k), piece)
                    out.append(remote(b, b, wp.at[0, i, k, kd], wp.at[1, i, k, kd], "dp", dp.up(kd)))
                    out[-1].start()
        return out

    def gather_c(i, ps):
        _, dst, hh = weights[i]
        for cp in ps:
            cp.wait_recv()
        wloads[i].wait()
        out = []
        for k in col.ks():
            out.append(remote(dst.at[hh], dst.at[hh], wc.at[0, i, k], wc.at[1, i, k], "col", col.up(k)))
            out[-1].start()
        return out

    z0 = gather_z(0)
    vz = [remote(vall.at[r], vall.at[r], vsem.at[0, k], vsem.at[1, k], "row", row.up(k)) for k in row.ks()]
    vc = [remote(qvall.at[c], qvall.at[c], vsem.at[2, k], vsem.at[3, k], "col", col.up(k)) for k in col.ks()]
    vc += [remote(uball.at[c], uball.at[c], vsem.at[4, k], vsem.at[5, k], "col", col.up(k)) for k in col.ks()]
    for cp in vz + vc:
        cp.start()
    loads[1].wait()

    def prep(i, carry):
        yacc[i, :SEQ] = cin[i].astype(F32)
        cb[i] = yacc[i].astype(BF16)
        return carry

    lax.fori_loop(0, NI, prep, 0)
    p0 = gather_p(0, z0)
    z1, z2 = gather_z(1), gather_z(2)
    for cp in vz + vc:
        cp.wait_recv()
    vec[...] = jnp.concatenate([vall[rr][:, :rows] for rr in range(R)], axis=1)
    g1, b1, ob, g2, b2, db = (vec[i:i + 1, :] for i in range(6))
    for hh in range(H):
        qb = qvall[hh // Hc][:, (hh % Hc) * E:(hh % Hc + 1) * E]
        zz = jnp.zeros((1, E), F32)
        bias3[hh] = jnp.concatenate([qb[0:1], zz, qb[1:2], zz], axis=1)
    ct[...] = cb[...].reshape(T, D).T
    c0 = gather_c(0, p0)
    for cp in c0:
        cp.wait_recv()
    wot[...] = jnp.concatenate([wa[hh][:, 3 * E:] for hh in range(H)], axis=1)

    key_ok = lax.broadcasted_iota(jnp.int32, (SP, SP), 0) < SEQ

    def fwd(i, carry):
        a = (xh1[i] * vec[0:1, :] + vec[1:2, :]).astype(BF16)
        a1[i] = a
        outs = []
        for hh in range(H):
            t = (mm(a, wa[hh], 1, 0) + bias3[hh]).astype(BF16)
            qkv[i, hh] = t
            q, k, v = t[:, :E], t[:, E:2 * E], t[:, 2 * E:3 * E]
            s = mm(k, q, 1, 1) * (LOG2E / math.sqrt(E))
            s = jnp.where(key_ok, s, -1e30)
            top = jnp.max(s, 0, keepdims=True)
            e = jnp.exp2(s - top)
            p = (e * (1.0 / rsum(e))).astype(BF16)
            pt[i, hh] = p
            outs.append(mm(p, v, 0, 0).astype(BF16))
        oo = jnp.concatenate(outs, axis=1)
        o[i] = oo
        hid = h[i] + mm(oo, wot[...], 1, 1) + vec[2:3, :]
        h[i] = hid
        xh, rstd = norm_parts(hid)
        xh2[i] = xh
        rs2[i] = rstd
        a2[i] = (xh * vec[3:4, :] + vec[4:5, :]).astype(BF16)
        yacc[i] = hid + vec[5:6, :]
        dacc[i] = jnp.zeros((SP, D), F32)
        return carry

    mid1, mid2 = (NI + 2) // 3, (2 * NI + 2) // 3
    lax.fori_loop(0, mid1, fwd, 0)
    p1, p2 = gather_p(1, z1), gather_p(2, z2)
    lax.fori_loop(mid1, mid2, fwd, 0)
    c1, c2 = gather_c(1, p1), gather_c(2, p2)
    lax.fori_loop(mid2, NI, fwd, 0)
    a2t[...] = a2[...].reshape(T, D).T
    for cp in c1 + c2:
        cp.wait_recv()

    redf = Reduce((rows, split), (dp, row, col), (f1, f2, f3, f4, f5, f6, f7), fsem)
    redt = Reduce((rows, split), (dp, row, col), (t1, t2, t3, t4, t5, t6, t7), tsem)

    def ff(half):
        w1, w2 = wup[half], wdn[half]
        bias = uball[half]

        def one(i, tot):
            u = mm(a2[i], w1, 1, 0) + bias
            act, slope = gelu_parts(u)
            gbi = act.astype(BF16)
            dd = mm(cb[i], w2, 1, 0) * slope
            dui = dd.astype(BF16)
            gb[i] = gbi
            du[i] = dui
            yacc[i] += mm(gbi, w2, 1, 1)
            dacc[i] += mm(dui, w1, 1, 1)
            return tot + rsum(dd)

        dubs[half] = lax.fori_loop(0, NI, one, jnp.zeros((1, FH), F32))
        return (mm(a2t[...], du[...].reshape(T, FH), 1, 0), mm(ct[...], gb[...].reshape(T, FH), 1, 0))

    for k in col.ks():
        for a, v in enumerate(ff(col.up(k))):
            redf.put_c(k, a, v)
        redf.start_c(k)
    mine = ff(c)
    redf.wait_c()
    for a, v in enumerate(mine):
        redf.put_p(a, v)
    redf.start_p()

    def mid(i, carry):
        s_db, s_g, s_b, s_ob = carry
        xin[i] = yacc[i][:SEQ].astype(BF16)
        cf = cb[i].astype(F32)
        da = dacc[i]
        xh = xh2[i]
        dh = cf + norm_back(da, vec[3:4, :], xh, rs2[i])
        h[i] = dh
        db_ = dh.astype(BF16)
        a2[i] = db_
        dd = mm(db_, wot[...], 1, 0).astype(BF16)
        for hh in range(H):
            dout[i, hh] = dd[:, hh * E:(hh + 1) * E]
        dacc[i] = jnp.zeros((SP, D), F32)
        return s_db + rsum(cf), s_g + rsum(da * xh), s_b + rsum(da), s_ob + rsum(dh)

    z = jnp.zeros((1, D), F32)
    s_db, s_g2, s_b2, s_ob = lax.fori_loop(0, NI, mid, (z, z, z, z))
    y_cp = pltpu.make_async_copy(xin, y_o, osem.at[0])
    y_cp.start()
    ct[...] = a2[...].reshape(T, D).T
    a2t[...] = a1[...].reshape(T, D).T
    dwo_all = mm(ct[...], o[...].reshape(T, D), 1, 0)
    for hh in range(H):
        dwo[hh] = dwo_all[:, hh * E:(hh + 1) * E]

    scale = 1.0 / math.sqrt(E)

    def back(hh):
        def one(i, tot):
            t = qkv[i, hh]
            q, k, v = t[:, :E], t[:, E:2 * E], t[:, 2 * E:3 * E]
            p = pt[i, hh]
            do = dout[i, hh]
            pf = p.astype(F32)
            dpr = mm(v, do, 1, 1)
            delta = rsum(pf * dpr)
            ds = (pf * (dpr - delta)).astype(BF16)
            dk = mm(ds, q, 1, 0) * scale
            dv = mm(p, do, 1, 0)
            dq = mm(ds, k, 0, 0) * scale
            dd = jnp.concatenate([dq, dk, dv, jnp.zeros((SP, E), F32)], axis=1)
            db_ = dd.astype(BF16)
            dqkv[i] = db_
            dacc[i] += mm(db_, wa[hh], 1, 1)
            return tot + rsum(dd)

        dqvs[hh] = lax.fori_loop(0, NI, one, jnp.zeros((1, W4), F32), unroll=True)
        g = mm(a2t[...], dqkv[...].reshape(T, W4), 1, 0)
        return jnp.concatenate([g[:, :3 * E], dwo[hh]], axis=1)

    for k in col.ks():
        def other(j, carry):
            redt.put_c(k, j, back(col.up(k) * Hc + j))
            return carry

        lax.fori_loop(0, Hc, other, 0)
        redt.start_c(k)
    redf.start_z()
    redt.wait_c()

    def mine_(j, carry):
        redt.put_p(j, back(c * Hc + j))
        return carry

    lax.fori_loop(0, Hc, mine_, 0)
    redt.start_p()
    redf.start_a()

    def last(i, carry):
        s_g, s_b = carry
        da = dacc[i]
        xh = xh1[i]
        dx = h[i] + norm_back(da, vec[0:1, :], xh, rs1[i])
        dxb[i] = dx[:SEQ]
        return s_g + rsum(da * xh), s_b + rsum(da)

    s_g1, s_b1 = lax.fori_loop(0, NI, last, (z, z))
    dx_cp = pltpu.make_async_copy(dxb, dx_o, osem.at[1])
    dx_cp.start()

    six = jnp.concatenate([s_g1, s_b1, s_ob, s_g2, s_b2, s_db], axis=0)
    nf = FH // 128
    for cc in range(C):
        tail = [jnp.concatenate([dqvs[cc * Hc + j][:, :E], dqvs[cc * Hc + j][:, 2 * E:3 * E]], axis=1) for j in range(Hc)]
        tail += [dubs[cc][:, j * 128:(j + 1) * 128] for j in range(nf)]
        tail = jnp.concatenate(tail, axis=0)
        for rr in range(R):
            sgs[cc, rr, 0:6, 0:rows] = six[:, rr * rows:(rr + 1) * rows]
            sgs[cc, rr, 6:6 + Hc + nf, 0:2 * E] = tail
    sgc[c] = sgs[c]
    gc = [remote(sgs.at[col.up(k)], sgc.at[c], gsem.at[0, k], gsem.at[1, k], "col", col.up(k)) for k in col.ks()]
    for cp in gc:
        cp.start()
    for cp in gc:
        cp.wait_recv()
    s = sgc[0]
    for k in range(1, C):
        s = s + sgc[k]
    sgp[d] = s
    gp = [remote(sgp.at[d], sgp.at[d], gsem.at[2, k], gsem.at[3, k], "dp", dp.up(k)) for k in dp.ks()]
    for cp in gp:
        cp.start()
    redt.start_z()
    for cp in gp:
        cp.wait_recv()
    s = sgp[0]
    for k in range(1, DP):
        s = s + sgp[k]
    sgz[...] = s
    sgr[r] = sgz[r]
    gz = [remote(sgz.at[row.up(k)], sgr.at[r], gsem.at[4, k], gsem.at[5, k], "row", row.up(k)) for k in row.ks()]
    for cp in gz:
        cp.start()

    def put_f(a, rs, ls, v):
        so_f[a, rs, ls] = v

    redf.finish(put_f)
    outs = [y_cp, dx_cp, pltpu.make_async_copy(so_f.at[0], dup_o, osem.at[2]), pltpu.make_async_copy(so_f.at[1], ddn_o, osem.at[3])]
    for cp in outs[2:]:
        cp.start()
    redt.start_a()
    for cp in gz:
        cp.wait_recv()
    s = sgr[0]
    for k in range(1, R):
        s = s + sgr[k]
    for j in range(Hc):
        dqvb_o[0:1, j * E:(j + 1) * E] = s[6 + j:7 + j, :E]
        dqvb_o[1:2, j * E:(j + 1) * E] = s[6 + j:7 + j, E:2 * E]
    for i, ref in enumerate([dg1_o, db1_o, dob_o, dg2_o, db2_o, ddb_o]):
        ref[...] = s[i:i + 1, :rows].reshape(rows)
    for j in range(nf):
        dub_o[pl.ds(j * 128, 128)] = s[6 + Hc + j:7 + Hc + j, :].reshape(128)

    def put_t(a, rs, ls, v):
        so_t[a, rs, ls] = v

    redt.finish(put_t)
    outs.append(pltpu.make_async_copy(so_t, daw_o, osem.at[11]))
    outs[-1].start()
    for cp in gc + gp + gz + vz + vc + z0 + z1 + z2 + p0 + p1 + p2 + c0 + c1 + c2:
        cp.wait_send()
    for cp in outs:
        cp.wait()


def pick_split(n, rows, widths):
    for sr in range(1, n + 1):
        if n % sr == 0 and rows % (16 * sr) == 0 and all(w % (128 * (n // sr)) == 0 for w in widths):
            return sr, n // sr
    return 1, 1


def local(sizes, x, g1, b1, aw, qvb, ob, g2, b2, up, ub, dn, db, c):
    DP, R, C = sizes
    NI, SEQ, D = x.shape
    Hc, rows, W4 = aw.shape
    E, FH = W4 // 4, up.shape[1]
    H, SP = C * Hc, -(-SEQ // 16) * 16
    T = NI * SP
    split = pick_split(DP, rows, (W4, FH))
    np_ = split[0] * split[1]
    pr, pw, pf = rows // split[0], W4 // split[1], FH // split[1]
    sd, vm = jax.ShapeDtypeStruct, pltpu.VMEM
    dma = pltpu.SemaphoreType.DMA
    nf = FH // 128
    S = -(-(6 + Hc + nf) // 8) * 8
    cfg = (DP, R, C, NI, SEQ, SP, D, Hc, E, FH, rows, split)

    def red(A, L, pl_):
        return [vm((C - 1, A, D, L), BF16)] * 2 + [vm((np_, R, A, pr, pl_), BF16), vm((DP, R, A, pr, pl_), BF16),
                vm((R, A, pr, pl_), BF16), vm((R, A, pr, pl_), BF16), vm((np_, A, pr, pl_), BF16)]

    scratch = [
        vm((H, D, W4), BF16), vm((C, D, FH), BF16), vm((C, D, FH), BF16), vm((R, 8, 128), F32),
        vm((C, 2, Hc * E), F32), vm((C, 1, FH), F32), vm((8, D), F32), vm((H, 1, W4), F32),
        vm((NI, SEQ, D), BF16), vm((NI, SEQ, D), BF16), vm((NI, SP, D), BF16), vm((NI, SP, D), F32), vm((NI, SP, 1), F32),
        vm((NI, SP, D), BF16), vm((NI, H, SP, W4), BF16), vm((NI, H, SP, SP), BF16), vm((NI, SP, D), BF16),
        vm((NI, SP, D), F32), vm((NI, SP, D), F32), vm((NI, SP, 1), F32), vm((NI, SP, D), BF16), vm((D, D), BF16),
        vm((NI, SP, FH), BF16), vm((NI, SP, FH), BF16), vm((NI, SP, D), F32), vm((NI, SP, D), F32),
        vm((NI, H, SP, E), BF16), vm((NI, SP, W4), BF16), vm((D, T), BF16), vm((D, T), BF16), vm((H, D, E), F32), vm((NI, SEQ, D), F32), vm((C, 1, FH), F32), vm((H, 1, W4), F32),
        *red(2, FH, pf), *red(Hc, W4, pw),
        vm((2, rows, FH), F32), vm((Hc, rows, W4), F32),
        vm((C, R, S, 128), F32), vm((C, R, S, 128), F32), vm((DP, R, S, 128), F32), vm((R, S, 128), F32),
        vm((R, S, 128), F32),
        dma((13,)), dma((12 + nf,)), dma((2, 3, R)), dma((2, 3, R, DP)), dma((2, 3, C)),
        dma((8, max(DP, R, C))), dma((8, max(DP, R, C))), dma((6, max(R, C))), dma((6, max(DP, R, C))),
    ]
    any_ = pl.BlockSpec(memory_space=pl.ANY)
    vm_ = pl.BlockSpec(memory_space=pltpu.VMEM)
    v = lambda a: sd(a.shape, F32)
    return tuple(pl.pallas_call(
        functools.partial(kernel, cfg),
        out_shape=(sd(x.shape, BF16), v(x), v(g1), v(b1), v(aw), v(qvb), v(ob), v(g2), v(b2), v(up), v(ub), v(dn), v(db)),
        in_specs=[any_, vm_, vm_, any_, vm_, vm_, vm_, vm_, any_, vm_, any_, vm_, any_],
        out_specs=[any_, any_, vm_, vm_, any_, vm_, vm_, vm_, vm_, any_, vm_, any_, vm_],
        scratch_shapes=scratch,
        compiler_params=pltpu.CompilerParams(vmem_limit_bytes=67043328, collective_id=0, has_side_effects=True),
    )(x, g1, b1, aw, qvb, ob, g2, b2, up, ub, dn, db, c))


def solution(mesh):
    sizes = tuple(mesh.shape[a] for a in ("dp", "row", "col"))
    placed = (
        P(("dp", "row", "col"), None, None),
        P("row"),
        P("row"),
        P("col", "row", None),
        P(None, "col"),
        P("row"),
        P("row"),
        P("row"),
        P("row", "col"),
        P("col"),
        P("row", "col"),
        P("row"),
        P(("dp", "row", "col"), None, None),
    )
    return jax.shard_map(
        functools.partial(local, sizes),
        mesh=mesh,
        in_specs=placed,
        out_specs=(
            P(("dp", "row", "col"), None, None),
            P(("dp", "row", "col"), None, None),
            P("row"),
            P("row"),
            P("col", "row", None),
            P(None, "col"),
            P("row"),
            P("row"),
            P("row"),
            P("row", "col"),
            P("col"),
            P("row", "col"),
            P("row"),
        ),
        check_vma=False,
    )
```

time: 338 us -> 114 us (0.34)
  waiting for transfers between devices: 124 us -> 0 us
  blocking collectives: 111 us -> 0 us
  Pallas kernels: 72.5 us -> 104 us
  between operations: 14.5 us -> 0.75 us
  other arithmetic: 12.6 us -> 0 us
  local copies, waits for them, and re-layouts: 3.67 us -> 10 us
    reduce_scatter x6 -> x0, waiting for transfers between devices: 117 us -> none  [the longest x3 86.2 us: scatter(): g = lax.psum_scatter(g, 'row', scatter_dimension=rdim, tiled=True)]
    all_gather x6 -> x0, blocking collectives: 69.9 us -> none  [the longest x4 66.3 us: local(): gr = lambda v, ax: lax.all_gather(v, 'row', axis=ax, tiled=True)]
    psum x1 -> x0, blocking collectives: 40.7 us -> none  [local(): lax.psum(jnp.concatenate([dg1[0], db1[0], dob[0], dg2[0], db2[0], ddb[0],...]
    pallas_call x1, Pallas kernels: 72.5 us -> 104 us  [local(): pl.pallas_call(functools.partial(kernel, cfg), out_shape=(sd(x.shape, BF1...]
    convert_element_type x4 -> x0, other arithmetic: 8.6 us -> none  [the longest x3 6.96 us: scatter(): g = g.astype(BF16)]
    unnamed x50 -> x37, local copies, waits for them, and re-layouts: 1.49 us -> 10 us
    psum x1 -> x0, waiting for transfers between devices: 6.82 us -> none  [scatter(): return lax.psum(g, 'dp').astype(F32)]
  transfers between devices with their start and end apart: 10 -> 0, of which waited for: 7 -> 0; matrix products, arithmetic and copies ran while one was open for 2% -> 0% of each run, Pallas kernels for 0% -> 0%
where the time goes in v2:
time: 114 us
  Pallas kernels  104 us (91%)
  local copies, waits for them, and re-layouts  10 us (9%)
    pallas_call x1, Pallas kernels, local(): pl.pallas_call(functools.partial(kernel, cfg), out_shape=(sd(x.shape, BF1...  104 us
    unnamed x37, local copies, waits for them, and re-layouts  10 us

profile of v2, /device:TPU:0, one launch (start us, length us, event | category | flops | bytes accessed | tf_op | source)
XLA Modules:
  0.0 114.3 jit_solution(9576429140838398436)
XLA Ops:
  0.6 103.6 %shard_map.228 = (bf16[6,197,384]{2,1,0:T(8,128)(2,1)}, f32[6,197,384]{2,1,0:T(8,128)}, f32[96]{0:T(128)}, f32[96]{0:T(128)}, f32[3,96,256]{2,1,0:T(8,128)}, /*i...) custom-call(bf16[6,197,384]{2,1,0:T(8,128)(2,1)} %refs_0_.1, ...), custom_call_target="tpu_custom_call" | custom-call | tf_op jit(solution)/shard_map/pallas_call | solution.py:543
  104.2 0.0 copy-start
  104.2 2.3 %copy.39 = bf16[6,197,384]{2,1,0:T(8,128)(2,1)} copy(bf16[6,197,384]{2,1,0:T(8,128)(2,1)} %get-tuple-element.26) | data formatting | bytes 1815552
  106.6 0.0 copy-start.5
  106.6 0.0 copy-start.9
  106.6 0.0 copy-start.8
  106.6 0.0 copy-start.7
  106.6 0.0 copy-start.2
  106.6 0.0 copy-start.4
  106.6 0.0 copy-start.1
  106.6 0.0 copy-start.6
  106.6 1.2 %copy.40 = f32[6,197,384]{2,1,0:T(8,128)} copy(f32[6,197,384]{2,1,0:T(8,128)S(1)} %copy-done) | data formatting | bytes 3631104
  107.9 0.5 copy.41
  108.4 0.5 copy.42
  108.9 0.7 copy.43
  109.6 0.6 copy.44
  110.2 0.5 copy.45
  110.7 0.0 copy-done.8
  110.7 0.5 copy.46
  111.2 0.5 copy.47
  111.8 0.7 copy.48
  112.5 0.6 copy.49
  113.1 0.7 copy.50
  113.8 0.5 copy.51
  (14 shorter events, 0.0 us)
Async XLA Ops:
  104.2 2.3 %copy-start = (f32[6,197,384]{2,1,0:T(8,128)S(1)}, f32[6,197,384]{2,1,0:T(8,128)}, u32[]{:S(2)}) copy-start(f32[6,197,384]{2,1,0:T(8,128)} %get-tuple-element.27) | copy-start | bytes 5446660
  106.6 1.3 %copy-start.11 = (f32[96]{0:T(128)S(1)}, f32[96]{0:T(128)}, u32[]{:S(2)}) copy-start(f32[96]{0:T(128)} %get-tuple-element.28) | copy-start | bytes 1156
  106.6 1.8 %copy-start.10 = (f32[96]{0:T(128)S(1)}, f32[96]{0:T(128)}, u32[]{:S(2)}) copy-start(f32[96]{0:T(128)} %get-tuple-element.29) | copy-start | bytes 1156
  106.6 2.4 %copy-start.3 = (f32[3,96,256]{2,1,0:T(8,128)S(1)}, f32[3,96,256]{2,1,0:T(8,128)}, u32[]{:S(2)}) copy-start(f32[3,96,256]{2,1,0:T(8,128)} %get-tuple-element.30) | copy-start | bytes 884740
  106.6 3.1 %copy-start.5 = (f32[2,192]{1,0:T(2,128)S(1)}, f32[2,192]{1,0:T(2,128)}, u32[]{:S(2)}) copy-start(f32[2,192]{1,0:T(2,128)} %get-tuple-element.31) | copy-start | bytes 4612
  106.6 3.6 %copy-start.9 = (f32[96]{0:T(128)S(1)}, f32[96]{0:T(128)}, u32[]{:S(2)}) copy-start(f32[96]{0:T(128)} %get-tuple-element.32) | copy-start | bytes 1156
  106.6 4.1 %copy-start.8 = (f32[96]{0:T(128)S(1)}, f32[96]{0:T(128)}, u32[]{:S(2)}) copy-start(f32[96]{0:T(128)} %get-tuple-element.33) | copy-start | bytes 1156
  106.6 4.6 %copy-start.7 = (f32[96]{0:T(128)S(1)}, f32[96]{0:T(128)}, u32[]{:S(2)}) copy-start(f32[96]{0:T(128)} %get-tuple-element.34) | copy-start | bytes 1156
  106.6 5.1 %copy-start.2 = (f32[96,768]{1,0:T(8,128)S(1)}, f32[96,768]{1,0:T(8,128)}, u32[]{:S(2)}) copy-start(f32[96,768]{1,0:T(8,128)} %get-tuple-element.35) | copy-start | bytes 884740
  106.6 5.9 %copy-start.4 = (f32[768]{0:T(1024)S(1)}, f32[768]{0:T(1024)}, u32[]{:S(2)}) copy-start(f32[768]{0:T(1024)} %get-tuple-element.36) | copy-start | bytes 9220
  106.6 6.4 %copy-start.1 = (f32[96,768]{1,0:T(8,128)S(1)}, f32[96,768]{1,0:T(8,128)}, u32[]{:S(2)}) copy-start(f32[96,768]{1,0:T(8,128)} %get-tuple-element.37) | copy-start | bytes 884740
  106.6 7.1 %copy-start.6 = (f32[96]{0:T(128)S(1)}, f32[96]{0:T(128)}, u32[]{:S(2)}) copy-start(f32[96]{0:T(128)} %get-tuple-element.38) | copy-start | bytes 1156

commit v3 on v2

v3 whole, which is shorter than its diff:
```python
import functools
import math

import jax
import jax.numpy as jnp
from jax import lax
from jax.experimental import pallas as pl
from jax.experimental.pallas import tpu as pltpu
from jax.sharding import PartitionSpec as P

EPS = 1e-06
ROOT_HALF = 0.7071067811865476
INV_ROOT_TWO_PI = 0.3989422804014327
LOG2E = 1.4426950408889634
F32, BF16 = jnp.float32, jnp.bfloat16
MESH = pl.DeviceIdType.MESH


def mm(a, b, ca, cb):
    return lax.dot_general(a, b, (((ca,), (cb,)), ((), ())), preferred_element_type=F32)


def norm_parts(v):
    mean = jnp.mean(v, -1, keepdims=True)
    cen = v - mean
    rstd = lax.rsqrt(jnp.mean(cen * cen, -1, keepdims=True) + EPS)
    return cen * rstd, rstd


def norm_back(g, gain, xhat, rstd):
    gx = g * gain
    return rstd * (gx - jnp.mean(gx, -1, keepdims=True) - xhat * jnp.mean(gx * xhat, -1, keepdims=True))


def gelu_parts(u):
    w = u * ROOT_HALF
    cdf = 0.5 + 0.5 * lax.erf(w)
    bell = jnp.exp2((w * w) * -LOG2E)
    return u * cdf, cdf + (w * bell) * (INV_ROOT_TWO_PI / ROOT_HALF)


SKIP = set()


def loop(lo, hi, body, init, **kw):
    return init if body.__name__ in SKIP else lax.fori_loop(lo, hi, body, init, **kw)


def rsum(v):
    return jnp.sum(v, 0, keepdims=True)


class Shift:
    def __init__(self, axis, n):
        self.axis, self.n, self.me = axis, n, lax.axis_index(axis)

    def up(self, k):
        return lax.rem(self.me + k, self.n)

    def down(self, k):
        return lax.rem(self.me + self.n - k, self.n)

    def ks(self):
        return range(1, self.n)


def remote(src, dst, ssem, rsem, axis, to):
    return pltpu.make_async_remote_copy(
        src_ref=src, dst_ref=dst, send_sem=ssem, recv_sem=rsem, device_id={axis: to}, device_id_type=MESH)


class Reduce:
    def __init__(self, cfg, ax, bufs, sems):
        self.rows, self.split = cfg
        self.dp, self.row, self.col = ax
        (self.sb, self.rc, self.rp, self.sz, self.rz, self.fin) = bufs
        self.sems = sems
        self.np = self.fin.shape[0]
        self.p, self.z, self.a = [], [], []

    def put(self, slot, a, v):
        sr, sl = self.split
        pr, pw = self.fin.shape[-2:]
        for r in range(self.row.n):
            for qr in range(sr):
                for ql in range(sl):
                    lo = r * self.rows + qr * pr
                    self.sb[slot, qr * sl + ql, r, a] = v[lo:lo + pr, ql * pw:(ql + 1) * pw].astype(BF16)

    def c(self, k):
        return remote(self.sb.at[k - 1], self.rc.at[k - 1], self.sems.at[0, k], self.sems.at[1, k], self.col.axis, self.col.up(k))

    def start_p(self):
        own = self.col.n - 1
        if own:
            t = self.sb[own].astype(F32)
            for k in self.col.ks():
                self.c(k).wait_recv()
                t = t + self.rc[k - 1].astype(F32)
            self.sb[own] = t.astype(BF16)
        if self.np == 1:
            self.rp[self.dp.me] = self.sb[own, 0]
        for k in self.dp.ks():
            to = self.dp.up(k)
            self.p.append(remote(self.sb.at[own, to if self.np > 1 else 0], self.rp.at[self.dp.me],
                                 self.sems.at[2, k], self.sems.at[3, k], self.dp.axis, to))
            self.p[-1].start()

    def start_z(self):
        for cp in self.p:
            cp.wait_recv()
        if self.np > 1:
            t = self.sb[self.col.n - 1, self.dp.me].astype(F32)
            for k in self.dp.ks():
                t = t + self.rp[self.dp.up(k)].astype(F32)
        else:
            t = self.rp[0].astype(F32)
            for q in range(1, self.dp.n):
                t = t + self.rp[q].astype(F32)
        self.sz[...] = t.astype(BF16)
        for k in self.row.ks():
            to = self.row.up(k)
            self.z.append(remote(self.sz.at[to], self.rz.at[self.row.me], self.sems.at[4, k], self.sems.at[5, k],
                                 self.row.axis, to))
            self.z[-1].start()

    def start_a(self):
        for cp in self.z:
            cp.wait_recv()
        t = self.sz[self.row.me].astype(F32)
        for k in self.row.ks():
            t = t + self.rz[self.row.up(k)].astype(F32)
        me = self.dp.me if self.np > 1 else 0
        self.fin[me] = t.astype(BF16)
        if self.np > 1:
            for k in self.dp.ks():
                self.a.append(remote(self.fin.at[me], self.fin.at[me], self.sems.at[6, k], self.sems.at[7, k],
                                     self.dp.axis, self.dp.up(k)))
                self.a[-1].start()

    def finish(self):
        for cp in self.a:
            cp.wait_recv()

    def drain(self):
        for k in self.col.ks():
            self.c(k).wait_send()
        for cp in self.p + self.z + self.a:
            cp.wait_send()


def kernel(cfg, *refs):
    (DP, R, C, NI, SEQ, SP, D, Hc, E, FH, rows, split, chunks) = cfg
    (x_hbm, g1_h, b1_h, aw_h, qvb_h, ob_h, g2_h, b2_h, up_h, ub_h, dn_h, db_h, c_hbm) = refs[:13]
    nc = len(chunks)
    (y_o, dx_o, ft_o, sg_o), ff_o = refs[13:17], refs[17:17 + nc]
    refs = refs[17 + nc:]
    fbuf = [refs[6 * i:6 * i + 6] for i in range(nc)]
    tbuf = [refs[6 * (nc + j):6 * (nc + j) + 6] for j in range(Hc)]
    (wa, wup, wdn, vall, qvall, uball, vec, bias3, xin, cin, cb, xh1, rs1, a1, qkv, pt, o, h, xh2, rs2, a2, wot, wotp,
     gb, du, yacc, dacc, dout, a2t, ct, a1t, dwo, dxb, dubs, dqvs,
     sgs, sgc, sgp, sgz, sgr, sgf,
     lsem, osem, wz, wp, wc, rsem, vsem, gsem) = refs[6 * (nc + Hc):]
    H, T, W4 = C * Hc, NI * SP, 4 * E
    dp, row, col = Shift("dp", DP), Shift("row", R), Shift("col", C)
    d, r, c = dp.me, row.me, col.me
    sr, sl = split
    np_ = sr * sl
    part = np_ > 1

    loads = [pltpu.make_async_copy(x_hbm, xin, lsem.at[0]), pltpu.make_async_copy(c_hbm, cin, lsem.at[1])]
    own = pl.ds(pl.multiple_of(r * rows, rows), rows)
    heads = pl.ds(c * Hc, Hc)
    wloads = [pltpu.make_async_copy(aw_h, wa.at[heads, own, :], lsem.at[10]),
              pltpu.make_async_copy(up_h, wup.at[c, own, :], lsem.at[11]),
              pltpu.make_async_copy(dn_h, wdn.at[c, own, :], lsem.at[12])]
    for cp in loads + wloads:
        cp.start()
    for i, v in enumerate([g1_h, b1_h, ob_h, g2_h, b2_h, db_h]):
        vall[r, i:i + 1, 0:rows] = v[...].reshape(1, rows)
    qvall[c] = qvb_h[...]
    uball[c] = ub_h[...].reshape(1, FH)

    barrier = pltpu.get_barrier_semaphore()
    for ax in (dp, row, col):
        for k in ax.ks():
            pl.semaphore_signal(barrier, inc=1, device_id={ax.axis: ax.up(k)}, device_id_type=MESH)

    xh1[:, SP - 16:, :] = jnp.zeros((NI, 16, D), F32)
    h[:, SP - 16:, :] = jnp.zeros((NI, 16, D), F32)
    yacc[:, SP - 16:, :] = jnp.zeros((NI, 16, D), F32)
    rs1[:, SP - 16:, :] = jnp.zeros((NI, 16, 1), F32)
    sgs[...] = jnp.zeros(sgs.shape, F32)
    loads[0].wait()

    def norm1(i, carry):
        xf = xin[i].astype(F32)
        xh, rstd = norm_parts(xf)
        xh1[i, :SEQ] = xh
        rs1[i, :SEQ] = rstd
        h[i, :SEQ] = xf
        return carry

    loop(0, NI, norm1, 0)
    pl.semaphore_wait(barrier, (DP - 1) + (R - 1) + (C - 1))

    piece = d if part else 0
    off = lax.rem(c * Hc, 2)
    order = [lax.rem(off + e, Hc) for e in range(Hc)]
    units = [(aw_h.at[j], wa.at[c * Hc + j]) for j in order]
    for lo, w in chunks:
        cut = (slice(None), pl.ds(lo, w))
        units += [(up_h.at[cut], wup.at[(c,) + cut]), (dn_h.at[cut], wdn.at[(c,) + cut])]

    def cut_of(ref, rr, q):
        pr, pw = rows // sr, ref.shape[1] // sl
        return ref.at[pl.ds(pl.multiple_of(rr * rows + (q // sl) * pr, pr), pr),
                      pl.ds(pl.multiple_of(lax.rem(q, sl) * pw, pw), pw)]

    def gather_z(u):
        src, dst = units[u]
        out = [remote(cut_of(src, 0, piece), cut_of(dst, r, piece), wz.at[0, u, k], wz.at[1, u, k], "row", row.up(k))
               for k in row.ks()]
        for cp in out:
            cp.start()
        return out

    def gather_p(u, zs):
        dst, out = units[u][1], []
        for cp, k in zip(zs, row.ks()):
            cp.wait_recv()
            if part:
                for kd in dp.ks():
                    b = cut_of(dst, row.down(k), piece)
                    out.append(remote(b, b, wp.at[0, u, k, kd], wp.at[1, u, k, kd], "dp", dp.up(kd)))
                    out[-1].start()
        return out

    def gather_c(u, ps):
        dst, out = units[u][1], []
        for cp in ps:
            cp.wait_recv()
        for k in col.ks():
            out.append(remote(dst, dst, wc.at[0, u, k], wc.at[1, u, k], "col", col.up(k)))
            out[-1].start()
        return out

    U = len(units)
    zs, ps, cs = [None] * U, [None] * U, [None] * U
    for u in range(Hc):
        zs[u] = gather_z(u)
    vz = [remote(vall.at[r], vall.at[r], vsem.at[0, k], vsem.at[1, k], "row", row.up(k)) for k in row.ks()]
    vc = [remote(qvall.at[c], qvall.at[c], vsem.at[2, k], vsem.at[3, k], "col", col.up(k)) for k in col.ks()]
    vc += [remote(uball.at[c], uball.at[c], vsem.at[4, k], vsem.at[5, k], "col", col.up(k)) for k in col.ks()]
    for cp in vz + vc:
        cp.start()
    loads[1].wait()

    def prep(i, carry):
        yacc[i, :SEQ] = cin[i].astype(F32)
        cb[i] = yacc[i].astype(BF16)
        return carry

    loop(0, NI, prep, 0)
    for u in range(Hc):
        ps[u] = gather_p(u, zs[u])
    for u in range(Hc, U):
        zs[u] = gather_z(u)
    for cp in vz + vc:
        cp.wait_recv()
    vec[...] = jnp.concatenate([vall[rr][:, :rows] for rr in range(R)], axis=1)
    for hh in range(H):
        qb = qvall[hh // Hc][:, (hh % Hc) * E:(hh % Hc + 1) * E]
        zz = jnp.zeros((1, E), F32)
        bias3[hh] = jnp.concatenate([zz, qb[0:1], qb[1:2], zz], axis=1)

    def act1(i, carry):
        a1[i] = (xh1[i] * vec[0:1, :] + vec[1:2, :]).astype(BF16)
        return carry

    loop(0, NI, act1, 0)
    ct[...] = cb[...].reshape(T, D).T
    for cp in wloads:
        cp.wait()
    first = min(2, Hc)
    for u in range(first):
        cs[u] = gather_c(u, ps[u])

    live = SEQ // 16 * 16
    key_ok = lax.broadcasted_iota(jnp.int32, (SP - live, SP), 0) < SEQ - live

    def attend(t):
        k, q, v = t[:, :E], t[:, E:2 * E], t[:, 2 * E:3 * E]
        s = mm(k, q, 1, 1)
        s = jnp.concatenate([s[:live], jnp.where(key_ok, s[live:], -1e30)], axis=0)
        top = jnp.max(s, 0, keepdims=True)
        e = jnp.exp2((s - top) * (LOG2E / math.sqrt(E)))
        p = (e * (1.0 / rsum(e))).astype(BF16)
        return p, mm(p, v, 0, 0).astype(BF16)

    def fwd(it, carry):
        pr = lax.rem((c * Hc + 1) // 2 + it, H // 2)
        a = a1[...].reshape(T, D)
        ts = []
        for hh in (2 * pr, 2 * pr + 1):
            w = wa[hh]
            w = jnp.concatenate([w[:, E:2 * E], w[:, :E], w[:, 2 * E:]], axis=1)
            t = (mm(a, w, 1, 0) + bias3[hh]).astype(BF16)
            qkv[hh] = t.reshape(NI, SP, W4)
            ts.append(t)
        for i in range(NI):
            outs = []
            for t, hh in zip(ts, (2 * pr, 2 * pr + 1)):
                p, oh = attend(t[i * SP:(i + 1) * SP])
                pt[hh, i] = p
                outs.append(oh)
            o[i, :, pl.ds(pl.multiple_of(pr * 2 * E, 2 * E), 2 * E)] = jnp.concatenate(outs, axis=1)
        return carry

    loop(0, 1, fwd, 0)
    for u in range(first, Hc):
        cs[u] = gather_c(u, ps[u])
    a1t[:D] = a1[...].reshape(T, D).T
    a1t[D:] = jnp.ones((16, T), BF16)
    a2t[D:] = jnp.ones((16, T), BF16)
    for u in range(Hc, Hc + 2):
        ps[u] = gather_p(u, zs[u])
    for u in range(Hc):
        for cp in cs[u]:
            cp.wait_recv()
    loop(1, H // 2, fwd, 0)
    for u in range(Hc + 2, U):
        ps[u] = gather_p(u, zs[u])
    wot[...] = jnp.concatenate([wa[hh][:, 3 * E:] for hh in range(H)], axis=1)
    for hh in range(H):
        wotp[:, hh * 2 * E:(hh + 1) * 2 * E] = jnp.concatenate([wa[hh][:, 3 * E:], jnp.zeros((D, E), BF16)], axis=1)

    G = math.gcd(NI, 3)
    GT = G * SP

    def proj(i, carry):
        im = pl.ds(i * G, G)
        back3 = lambda v: v.reshape(G, SP, D)
        hid = h[im].reshape(GT, D) + mm(o[im].reshape(GT, D), wot[...], 1, 1) + vec[2:3, :]
        h[im] = back3(hid)
        xh, rstd = norm_parts(hid)
        xh2[im] = back3(xh)
        rs2[im] = rstd.reshape(G, SP, 1)
        a2[im] = back3((xh * vec[3:4, :] + vec[4:5, :]).astype(BF16))
        yacc[im] = back3(hid + vec[5:6, :])
        return carry

    loop(0, NI // G, proj, 0)
    a2t[:D] = a2[...].reshape(T, D).T

    ax = (dp, row, col)
    redf = [Reduce((rows, split), ax, fbuf[i], rsem.at[i]) for i in range(nc)]
    redt = [Reduce((rows, split), ax, tbuf[j], rsem.at[nc + j]) for j in range(Hc)]

    def ff(half, lo, w, first):
        w1, w2 = wup[half, :, lo:lo + w], wdn[half, :, lo:lo + w]
        bias = uball[half, :, lo:lo + w]

        def ffone(i, carry):
            im = pl.ds(i * G, G)
            u = mm(a2[im].reshape(GT, D), w1, 1, 0) + bias
            act, slope = gelu_parts(u)
            gbi = act.astype(BF16)
            dui = (mm(cb[im].reshape(GT, D), w2, 1, 0) * slope).astype(BF16)
            gb[im, :, :w] = gbi.reshape(G, SP, w)
            du[im, :, :w] = dui.reshape(G, SP, w)
            yacc[im] += mm(gbi, w2, 1, 1).reshape(G, SP, D)
            dd = mm(dui, w1, 1, 1).reshape(G, SP, D)
            dacc[im] = dd if first else dacc[im] + dd
            return carry

        loop(0, NI // G, ffone, 0)
        gu = mm(a2t[...], du[:, :, :w].reshape(T, w), 1, 0)
        dubs[half, :, lo:lo + w] = gu[D:D + 1]
        return gu[:D], mm(ct[...], gb[:, :, :w].reshape(T, w), 1, 0)

    for i, (lo, w) in enumerate(chunks):
        if i == 0:
            for u in (Hc, Hc + 1):
                cs[u] = gather_c(u, ps[u])
        for a, v in enumerate(ff(c, lo, w, i == 0)):
            redf[i].put(C - 1, a, v)
        if i == 0:
            for u in range(Hc + 2, U):
                cs[u] = gather_c(u, ps[u])
        else:
            redf[i - 1].start_p()
        for u in (Hc + 2 * i, Hc + 2 * i + 1):
            for cp in cs[u]:
                cp.wait_recv()
        for k in col.ks():
            for a, v in enumerate(ff(col.up(k), lo, w, False)):
                redf[i].put(k - 1, a, v)
            redf[i].c(k).start()

    def mid(i, carry):
        s_db, s_g, s_b, s_ob = carry
        im = pl.ds(i * G, G)
        for j in range(G):
            xin[i * G + j] = yacc[i * G + j][:SEQ].astype(BF16)
        cf = cb[im].reshape(GT, D).astype(F32)
        da = dacc[im].reshape(GT, D)
        xh = xh2[im].reshape(GT, D)
        dh = cf + norm_back(da, vec[3:4, :], xh, rs2[im].reshape(GT, 1))
        h[im] = dh.reshape(G, SP, D)
        db_ = dh.astype(BF16)
        a2[im] = db_.reshape(G, SP, D)
        dd = mm(db_, wotp[...], 1, 0).astype(BF16)
        for hh in range(H):
            dout[hh, im] = dd[:, hh * 2 * E:(hh + 1) * 2 * E].reshape(G, SP, 2 * E)
        return s_db + rsum(cf), s_g + rsum(da * xh), s_b + rsum(da), s_ob + rsum(dh)

    z = jnp.zeros((1, D), F32)
    s_db, s_g2, s_b2, s_ob = loop(0, NI // G, mid, (z, z, z, z))
    y_cp = pltpu.make_async_copy(xin, y_o, osem.at[0])
    y_cp.start()
    ct[...] = a2[...].reshape(T, D).T
    dwo_all = mm(ct[...], o[...].reshape(T, D), 1, 0)
    for hh in range(H):
        dwo[hh] = jnp.concatenate([jnp.zeros((D, E), F32), dwo_all[:, hh * E:(hh + 1) * E]], axis=1)
    redf[nc - 1].start_p()

    low = lax.broadcasted_iota(jnp.int32, (SP, 2 * E), 1) < E

    def back(hh):
        if "back" not in SKIP:
            for i in range(NI):
                kq, v = qkv[hh, i, :, :2 * E], qkv[hh, i, :, 2 * E:]
                p = pt[hh, i]
                do = dout[hh, i]
                pf = p.astype(F32)
                dpr = mm(v * (1.0 / math.sqrt(E)), do, 1, 1)
                delta = rsum(pf * dpr)
                ds = (pf * (dpr - delta)).astype(BF16)
                dk = mm(ds, kq, 1, 0)
                dq = mm(ds, kq, 0, 0)
                dv = mm(p, do, 1, 0)
                qkv[hh, i, :, :2 * E] = jnp.where(low, dq, dk).astype(BF16)
                qkv[hh, i, :, 2 * E:] = dv.astype(BF16)
        g = mm(a1t[...], qkv[hh].reshape(T, W4), 1, 0)
        dqvs[hh] = g[D:D + 1]
        return jnp.concatenate([g[:D, :2 * E], g[:D, 2 * E:] + dwo[hh]], axis=1)

    steps = [lambda: redf[0].start_z(),
             lambda: (redf[0].start_a(), redf[-1].start_z() if nc > 1 else None, redt[0].start_z()),
             lambda: (redf[-1].start_a() if nc > 1 else None, redt[0].start_a(), redt[1].start_z())]
    for j in range(Hc):
        def pair(s, carry):
            redt[j].put(s, 0, back(lax.rem(c + 1 + s, C) * Hc + j))

            @pl.when(s < C - 1)
            def _():
                redt[j].c(s + 1).start()

            return carry

        lax.fori_loop(0, C, pair, 0)
        redt[j].start_p()
        if j < len(steps):
            steps[j]()

    def last(i, carry):
        s_g, s_b = carry
        im = pl.ds(i * G, G)
        da = mm(qkv[0, im].reshape(GT, W4), wa[0], 1, 1)
        for hh in range(1, H):
            da = da + mm(qkv[hh, im].reshape(GT, W4), wa[hh], 1, 1)
        xh = xh1[im].reshape(GT, D)
        dx = h[im].reshape(GT, D) + norm_back(da, vec[0:1, :], xh, rs1[im].reshape(GT, 1))
        for j in range(G):
            dxb[i * G + j] = dx[j * SP:j * SP + SEQ]
        return s_g + rsum(da * xh), s_b + rsum(da)

    s_g1, s_b1 = loop(0, NI // G, last, (z, z))
    dx_cp = pltpu.make_async_copy(dxb, dx_o, osem.at[1])
    dx_cp.start()

    six = jnp.concatenate([s_g1, s_b1, s_ob, s_g2, s_b2, s_db], axis=0)
    nf = FH // 128
    for cc in range(C):
        tail = [jnp.concatenate([dqvs[cc * Hc + j][:, :E], dqvs[cc * Hc + j][:, 2 * E:3 * E]], axis=1) for j in range(Hc)]
        tail += [dubs[cc][:, j * 128:(j + 1) * 128] for j in range(nf)]
        tail = jnp.concatenate(tail, axis=0)
        for rr in range(R):
            sgs[cc, rr, 0:6, 0:rows] = six[:, rr * rows:(rr + 1) * rows]
            sgs[cc, rr, 6:6 + Hc + nf, 0:128] = tail
    sgc[c] = sgs[c]
    gc = [remote(sgs.at[col.up(k)], sgc.at[c], gsem.at[0, k], gsem.at[1, k], "col", col.up(k)) for k in col.ks()]
    for cp in gc:
        cp.start()
    for cp in gc:
        cp.wait_recv()
    s = sgc[0]
    for k in range(1, C):
        s = s + sgc[k]
    sgp[d] = s
    gp = [remote(sgp.at[d], sgp.at[d], gsem.at[2, k], gsem.at[3, k], "dp", dp.up(k)) for k in dp.ks()]
    for cp in gp:
        cp.start()
    redt[Hc - 1].start_z()
    for cp in gp:
        cp.wait_recv()
    s = sgp[0]
    for k in range(1, DP):
        s = s + sgp[k]
    sgz[...] = s
    sgr[r] = sgz[r]
    gz = [remote(sgz.at[row.up(k)], sgr.at[r], gsem.at[4, k], gsem.at[5, k], "row", row.up(k)) for k in row.ks()]
    for cp in gz:
        cp.start()

    outs = [y_cp, dx_cp]
    if Hc > 1:
        redt[Hc - 2].start_a()
    for i in range(nc):
        redf[i].finish()
        outs.append(pltpu.make_async_copy(redf[i].fin, ff_o[i], osem.at[2 + i]))
        outs[-1].start()
    redt[Hc - 1].start_a()
    for cp in gz:
        cp.wait_recv()
    s = sgr[0]
    for k in range(1, R):
        s = s + sgr[k]
    sgf[...] = s
    outs.append(pltpu.make_async_copy(sgf, sg_o, osem.at[2 + nc]))
    outs[-1].start()
    for j in range(Hc):
        redt[j].finish()
        outs.append(pltpu.make_async_copy(redt[j].fin, ft_o.at[j], osem.at[3 + nc + j]))
        outs[-1].start()
    for red in redf + redt:
        red.drain()
    for cp in sum([x for x in zs + ps + cs if x], []):
        cp.wait_send()
    for cp in gc + gp + gz + vz + vc:
        cp.wait_send()
    for cp in outs:
        cp.wait()


def finish_kernel(cfg, *refs):
    rows, Hc, E, nf, (sr, sl), chunks = cfg
    nc = len(chunks)
    (y_i, dx_i, ft_i, sg_i), ff_i, refs = refs[:4], refs[4:4 + nc], refs[4 + nc:]
    (y_o, dx_o, dg1_o, db1_o, daw_o, dqvb_o, dob_o, dg2_o, db2_o, dup_o, dub_o, ddn_o, ddb_o) = refs[:13]
    (ybuf, xbuf, ft, sg, wf, wt, isem, osem), ff = refs[13:21], refs[21:]
    n = ybuf.shape[0]
    small = [pltpu.make_async_copy(i, v, isem.at[2 * n + k]) for k, (i, v) in enumerate(((sg_i, sg), (ft_i, ft), *zip(ff_i, ff)))]
    ins = [pltpu.make_async_copy(dx_i.at[k], xbuf.at[k], isem.at[k]) for k in range(n)]
    ins += [pltpu.make_async_copy(y_i.at[k], ybuf.at[k], isem.at[n + k]) for k in range(n)]
    outs = [pltpu.make_async_copy(xbuf.at[k], dx_o.at[k], osem.at[k]) for k in range(n)]
    outs += [pltpu.make_async_copy(ybuf.at[k], y_o.at[k], osem.at[n + k]) for k in range(n)]
    for cp in small + ins:
        cp.start()
    small[0].wait()
    s = sg[...]
    for i, ref in enumerate([dg1_o, db1_o, dob_o, dg2_o, db2_o, ddb_o]):
        ref[...] = s[i:i + 1, :rows].reshape(rows)
    for j in range(nf):
        dub_o[pl.ds(j * 128, 128)] = s[6 + Hc + j:7 + Hc + j, :128].reshape(128)
    for j in range(Hc):
        dqvb_o[0:1, j * E:(j + 1) * E] = s[6 + j:7 + j, :E]
        dqvb_o[1:2, j * E:(j + 1) * E] = s[6 + j:7 + j, E:2 * E]

    def lay(src, a, ref, lo):
        pr, pw = src.shape[-2:]
        for qr in range(sr):
            for ql in range(sl):
                ref[pl.ds(qr * pr, pr), pl.ds(lo + ql * pw, pw)] = src[qr * sl + ql, a].astype(F32)

    small[1].wait()
    for j in range(Hc):
        lay(ft.at[j], 0, wt.at[j], 0)
    for i, (lo, w) in enumerate(chunks):
        small[2 + i].wait()
        for a in range(2):
            lay(ff[i], a, wf.at[a], lo)
    big = [pltpu.make_async_copy(b, o, osem.at[2 * n + k]) for k, (b, o) in enumerate(((wf.at[0], dup_o), (wf.at[1], ddn_o), (wt, daw_o)))]
    for o in big:
        o.start()
    outs += big
    for i, o in zip(ins, outs):
        i.wait()
        o.start()
    for o in outs:
        o.wait()


def pick_split(n, rows, widths):
    for sr in range(1, n + 1):
        if n % sr == 0 and rows % (16 * sr) == 0 and all(w % (128 * (n // sr)) == 0 for w in widths):
            return sr, n // sr
    return 1, 1


def local(sizes, x, g1, b1, aw, qvb, ob, g2, b2, up, ub, dn, db, c):
    DP, R, C = sizes
    NI, SEQ, D = x.shape
    Hc, rows, W4 = aw.shape
    E, FH = W4 // 4, up.shape[1]
    H, SP = C * Hc, -(-SEQ // 16) * 16
    T = NI * SP
    chunks = ((0, FH - 256), (FH - 256, 256)) if FH % 256 == 0 and FH > 256 else ((0, FH),)
    nc, wmax = len(chunks), max(w for _, w in chunks)
    split = pick_split(DP, rows, (W4,) + tuple(w for _, w in chunks))
    np_ = split[0] * split[1]
    pr, pw = rows // split[0], W4 // split[1]
    sd, vm = jax.ShapeDtypeStruct, pltpu.VMEM
    dma = pltpu.SemaphoreType.DMA
    nf, VW = FH // 128, -(-rows // 128) * 128
    S = -(-(6 + Hc + nf) // 8) * 8
    cfg = (DP, R, C, NI, SEQ, SP, D, Hc, E, FH, rows, split, chunks)

    def red(A, L):
        pw = L // split[1]
        return [vm((C, np_, R, A, pr, pw), BF16), vm((max(C - 1, 1), np_, R, A, pr, pw), BF16), vm((DP, R, A, pr, pw), BF16),
                vm((R, A, pr, pw), BF16), vm((R, A, pr, pw), BF16), vm((np_, A, pr, pw), BF16)]

    scratch = sum([red(2, w) for _, w in chunks] + [red(1, W4)] * Hc, []) + [
        vm((H, D, W4), BF16), vm((C, D, FH), BF16), vm((C, D, FH), BF16), vm((R, 8, VW), F32),
        vm((C, 2, Hc * E), F32), vm((C, 1, FH), F32), vm((8, D), F32), vm((H, 1, W4), F32),
        vm((NI, SEQ, D), BF16), vm((NI, SEQ, D), BF16), vm((NI, SP, D), BF16), vm((NI, SP, D), F32), vm((NI, SP, 1), F32),
        vm((NI, SP, D), BF16), vm((H, NI, SP, W4), BF16), vm((H, NI, SP, SP), BF16), vm((NI, SP, D), BF16),
        vm((NI, SP, D), F32), vm((NI, SP, D), F32), vm((NI, SP, 1), F32), vm((NI, SP, D), BF16), vm((D, D), BF16),
        vm((D, 2 * D), BF16),
        vm((NI, SP, wmax), BF16), vm((NI, SP, wmax), BF16), vm((NI, SP, D), F32), vm((NI, SP, D), F32),
        vm((H, NI, SP, 2 * E), BF16), vm((D + 16, T), BF16), vm((D, T), BF16), vm((D + 16, T), BF16),
        vm((H, D, 2 * E), F32), vm((NI, SEQ, D), F32), vm((C, 1, FH), F32), vm((H, 1, W4), F32),
        vm((C, R, S, VW), F32), vm((C, R, S, VW), F32), vm((DP, R, S, VW), F32), vm((R, S, VW), F32),
        vm((R, S, VW), F32), vm((S, VW), F32),
        dma((13,)), dma((3 + nc + Hc,)), dma((2, Hc + 2 * nc, R)), dma((2, Hc + 2 * nc, R, DP)), dma((2, Hc + 2 * nc, C)),
        dma((nc + Hc, 8, max(DP, R, C))), dma((6, max(R, C))), dma((6, max(DP, R, C))),
    ]
    any_ = pl.BlockSpec(memory_space=pl.ANY)
    vm_ = pl.BlockSpec(memory_space=pltpu.VMEM)
    v = lambda a: sd(a.shape, F32)
    y, dx, ft, sg, *ff = pl.pallas_call(
        functools.partial(kernel, cfg),
        out_shape=(sd(x.shape, BF16), v(x), sd((Hc, np_, 1, pr, pw), BF16), sd((S, VW), F32),
                   *[sd((np_, 2, pr, w // split[1]), BF16) for _, w in chunks]),
        in_specs=[any_, vm_, vm_, any_, vm_, vm_, vm_, vm_, any_, vm_, any_, vm_, any_],
        out_specs=[any_] * (4 + nc),
        scratch_shapes=scratch,
        compiler_params=pltpu.CompilerParams(vmem_limit_bytes=67043328, collective_id=0, has_side_effects=True),
    )(x, g1, b1, aw, qvb, ob, g2, b2, up, ub, dn, db, c)
    return tuple(pl.pallas_call(
        functools.partial(finish_kernel, (rows, Hc, E, nf, split, chunks)),
        out_shape=(sd(x.shape, BF16), v(x), v(g1), v(b1), v(aw), v(qvb), v(ob), v(g2), v(b2), v(up), v(ub), v(dn), v(db)),
        in_specs=[any_] * (4 + nc),
        out_specs=[any_, any_, vm_, vm_, any_, vm_, vm_, vm_, vm_, any_, vm_, any_, vm_],
        scratch_shapes=[vm(x.shape, BF16), vm(x.shape, F32), vm(ft.shape, BF16), vm(sg.shape, F32),
                        vm((2, rows, FH), F32), vm(aw.shape, F32), dma((2 * NI + 2 + nc,)), dma((2 * NI + 3,)),
                        *[vm(f.shape, BF16) for f in ff]],
        compiler_params=pltpu.CompilerParams(vmem_limit_bytes=67043328),
    )(y, dx, ft, sg, *ff))


def solution(mesh):
    sizes = tuple(mesh.shape[a] for a in ("dp", "row", "col"))
    placed = (
        P(("dp", "row", "col"), None, None),
        P("row"),
        P("row"),
        P("col", "row", None),
        P(None, "col"),
        P("row"),
        P("row"),
        P("row"),
        P("row", "col"),
        P("col"),
        P("row", "col"),
        P("row"),
        P(("dp", "row", "col"), None, None),
    )
    return jax.shard_map(
        functools.partial(local, sizes),
        mesh=mesh,
        in_specs=placed,
        out_specs=(
            P(("dp", "row", "col"), None, None),
            P(("dp", "row", "col"), None, None),
            P("row"),
            P("row"),
            P("col", "row", None),
            P(None, "col"),
            P("row"),
            P("row"),
            P("row"),
            P("row", "col"),
            P("col"),
            P("row", "col"),
            P("row"),
        ),
        check_vma=False,
    )
```

time: 114 us -> 83.7 us (0.73)
  Pallas kernels: 104 us -> 82.6 us
  local copies, waits for them, and re-layouts: 10 us -> 0 us
    pallas_call x1, Pallas kernels: 104 us -> 78.8 us  [local(): pl.pallas_call(functools.partial(kernel, cfg), out_shape=(sd(x.shape, BF1...]
    unnamed x37 -> x0, local copies, waits for them, and re-layouts: 10 us -> none
    pallas_call x0 -> x1, Pallas kernels: none -> 3.79 us  [local(): pl.pallas_call(functools.partial(finish_kernel, (rows, Hc, E, nf, split,...]
where the time goes in v3:
time: 83.7 us; the launch traced here: 83.5 us
  Pallas kernels  82.6 us (99%)
    pallas_call x1, Pallas kernels, local(): pl.pallas_call(functools.partial(kernel, cfg), out_shape=(sd(x.shape, BF1...  78.8 us
    pallas_call x1, Pallas kernels, local(): pl.pallas_call(functools.partial(finish_kernel, (rows, Hc, E, nf, split,...  3.79 us

profile of v3, /device:TPU:0, one launch (start us, length us, event | category | flops | bytes accessed | tf_op | source)
XLA Modules:
  0.0 83.5 jit_solution(10721488369718492934)
XLA Ops:
  0.6 78.8 %shard_map.228 = (bf16[6,197,384]{2,1,0:T(8,128)(2,1)}, f32[6,197,384]{2,1,0:T(8,128)}, bf16[3,4,1,48,128]{4,3,2,1,0:T(8,128)(2,1)}, f32[16,128]{1,0:T(8,128)}, ...) custom-call(bf16[6,197,384]{2,1,0:T(8,128)(2,1)} %refs_0_.1, f32[96]{0:T(128)} %refs_1_.1, f32[96]{0:T(128)} %refs_2_.1, ...), custom_call_target="tpu_custom_call" | custom-call | tf_op jit(solution)/shard_map/pallas_call | solution.py:643
  79.5 3.8 %shard_map.229 = (bf16[6,197,384]{2,1,0:T(8,128)(2,1)}, f32[6,197,384]{2,1,0:T(8,128)}, f32[96]{0:T(128)}, f32[96]{0:T(128)}, f32[3,96,256]{2,1,0:T(8,128)}, /*i...) custom-call(bf16[6,197,384]{2,1,0:T(8,128)(2,1)} %get-tuple-element., ...), custom_call_target="tpu_custom_call" | custom-call | tf_op jit(solution)/shard_map/pallas_call | solution.py:652

commit v4 on v3

v4 whole, which is shorter than its diff:
```python
import functools
import math

import jax
import jax.numpy as jnp
from jax import lax
from jax.experimental import pallas as pl
from jax.experimental.pallas import tpu as pltpu
from jax.sharding import PartitionSpec as P

EPS = 1e-06
ROOT_HALF = 0.7071067811865476
INV_ROOT_TWO_PI = 0.3989422804014327
LOG2E = 1.4426950408889634
F32, BF16 = jnp.float32, jnp.bfloat16
MESH = pl.DeviceIdType.MESH


def mm(a, b, ca, cb):
    return lax.dot_general(a, b, (((ca,), (cb,)), ((), ())), preferred_element_type=F32)


def norm_parts(v):
    mean = jnp.mean(v, -1, keepdims=True)
    cen = v - mean
    rstd = lax.rsqrt(jnp.mean(cen * cen, -1, keepdims=True) + EPS)
    return cen * rstd, rstd


def norm_back(g, gain, xhat, rstd):
    gx = g * gain
    return rstd * (gx - jnp.mean(gx, -1, keepdims=True) - xhat * jnp.mean(gx * xhat, -1, keepdims=True))


def gelu_parts(u):
    w = u * ROOT_HALF
    cdf = 0.5 + 0.5 * lax.erf(w)
    bell = jnp.exp2((w * w) * -LOG2E)
    return u * cdf, cdf + (w * bell) * (INV_ROOT_TWO_PI / ROOT_HALF)


SKIP = set()


def loop(lo, hi, body, init, **kw):
    return init if body.__name__ in SKIP else lax.fori_loop(lo, hi, body, init, **kw)


def rsum(v):
    return jnp.sum(v, 0, keepdims=True)


def fold(v):
    t = v[:8]
    for lo in range(8, v.shape[0], 8):
        t = t + v[lo:lo + 8]
    return t


class Shift:
    def __init__(self, axis, n):
        self.axis, self.n, self.me = axis, n, lax.axis_index(axis)

    def up(self, k):
        return lax.rem(self.me + k, self.n)

    def down(self, k):
        return lax.rem(self.me + self.n - k, self.n)

    def ks(self):
        return range(1, self.n)


def remote(src, dst, ssem, rsem, axis, to):
    return pltpu.make_async_remote_copy(
        src_ref=src, dst_ref=dst, send_sem=ssem, recv_sem=rsem, device_id={axis: to}, device_id_type=MESH)


def settle(sem, region):
    pltpu.make_async_copy(region, region, sem).wait()


class Reduce:
    def __init__(self, cfg, ax, bufs, sems, halve):
        self.rows, self.split = cfg
        self.dp, self.row, self.col = ax
        (self.sb, self.rc, self.rp, self.sz, self.rz, self.fin) = bufs
        self.sems = sems
        self.np = self.fin.shape[0]
        self.halve = halve and self.np == 4
        self.own = self.col.n - 1

    def put(self, slot, a, v):
        sr, sl = self.split
        pr, pw = self.fin.shape[-2:]
        for r in range(self.row.n):
            for qr in range(sr):
                for ql in range(sl):
                    lo = r * self.rows + qr * pr
                    self.sb[slot, qr * sl + ql, a, r] = v[lo:lo + pr, ql * pw:(ql + 1) * pw].astype(BF16)

    def copy(self, src, dst, stage, ax, to):
        return remote(src, dst, self.sems.at[0, stage], self.sems.at[1, stage], ax.axis, to)

    def c(self, k):
        return self.copy(self.sb.at[k - 1], self.rc.at[k - 1], 0, self.col, self.col.up(k))

    def wait(self, side, stage):
        n, m = self.dp.n - 1, self.row.n - 1
        live = (self.own, n, self.halve, m, n and self.np > 1)[stage]
        if live:
            region = (lambda: self.rc, lambda: self.rp.at[0:2 if self.halve else n], lambda: self.rp.at[2],
                      lambda: self.rz.at[0:m], lambda: self.fin.at[0:n])[stage]
            settle(self.sems.at[side, stage], region())

    def halves(self, a):
        lo, hi = lax.rem(self.dp.me, 2), self.dp.me // 2
        if a % 2 == 0:
            return lo, hi, lambda x, y: x + 2 * y, self.dp.me + 1 - 2 * lo, self.dp.me + 2 - 4 * hi
        return hi, lo, lambda x, y: 2 * x + y, self.dp.me + 2 - 4 * hi, self.dp.me + 1 - 2 * lo

    def arrays(self):
        return range(self.fin.shape[1])

    def ps(self):
        if not self.halve:
            return [self.copy(self.sb.at[self.own, self.dp.up(k) if self.np > 1 else 0], self.rp.at[self.dp.me], 1,
                              self.dp, self.dp.up(k)) for k in self.dp.ks()]
        out = []
        for a in self.arrays():
            bit, _, at, to, _ = self.halves(a)
            for i in range(2):
                out.append(self.copy(self.sb.at[self.own, at(1 - bit, i), a], self.rp.at[i, a], 1, self.dp, to))
        return out

    def qs(self):
        out = []
        for a in self.arrays() if self.halve else ():
            bit, other, at, _, to = self.halves(a)
            out.append(self.copy(self.sb.at[self.own, at(bit, 1 - other), a], self.rp.at[2, a], 2, self.dp, to))
        return out

    def zs(self):
        return [self.copy(self.sz.at[self.row.up(k)], self.rz.at[self.row.me], 3, self.row, self.row.up(k))
                for k in self.row.ks()]

    def as_(self):
        if self.np == 1:
            return []
        mine = self.fin.at[self.dp.me]
        return [self.copy(mine, mine, 4, self.dp, self.dp.up(k)) for k in self.dp.ks()]

    def start_p(self):
        if self.own:
            self.wait(1, 0)
            t = self.sb[self.own].astype(F32)
            for k in self.col.ks():
                t = t + self.rc[k - 1].astype(F32)
            self.sb[self.own] = t.astype(BF16)
        if self.np == 1:
            self.rp[self.dp.me] = self.sb[self.own, 0]
        for cp in self.ps():
            cp.start()

    def start_q(self):
        if self.halve:
            self.wait(1, 1)
            for a in self.arrays():
                bit, other, at, _, _ = self.halves(a)
                q = at(bit, 1 - other)
                t = self.sb[self.own, q, a].astype(F32) + self.rp[1 - other, a].astype(F32)
                self.sb[self.own, q, a] = t.astype(BF16)
            for cp in self.qs():
                cp.start()

    def start_z(self):
        self.wait(1, 2 if self.halve else 1)
        for a in self.arrays():
            if self.halve:
                _, other, _, _, _ = self.halves(a)
                t = self.sb[self.own, self.dp.me, a].astype(F32) + self.rp[other, a].astype(F32) + self.rp[2, a].astype(F32)
            elif self.np > 1:
                t = self.sb[self.own, self.dp.me, a].astype(F32)
                for k in self.dp.ks():
                    t = t + self.rp[self.dp.up(k), a].astype(F32)
            else:
                t = self.rp[0, a].astype(F32)
                for q in range(1, self.dp.n):
                    t = t + self.rp[q, a].astype(F32)
            self.sz[:, a] = t.astype(BF16)
        for cp in self.zs():
            cp.start()

    def start_a(self):
        self.wait(1, 3)
        t = self.sz[self.row.me].astype(F32)
        for k in self.row.ks():
            t = t + self.rz[self.row.up(k)].astype(F32)
        self.fin[self.dp.me if self.np > 1 else 0] = t.astype(BF16)
        for cp in self.as_():
            cp.start()

    def finish(self):
        self.wait(1, 4)

    def drain(self):
        for stage in range(5):
            self.wait(0, stage)


def kernel(cfg, *refs):
    (DP, R, C, NI, SEQ, SP, D, Hc, E, FH, rows, split, chunks) = cfg
    (x_hbm, g1_h, b1_h, aw_h, qvb_h, ob_h, g2_h, b2_h, up_h, ub_h, dn_h, db_h, c_hbm) = refs[:13]
    nc = len(chunks)
    (y_o, dx_o, ft_o, sg_o), ff_o = refs[13:17], refs[17:17 + nc]
    refs = refs[17 + nc:]
    fbuf = [refs[6 * i:6 * i + 6] for i in range(nc)]
    tbuf = [refs[6 * (nc + j):6 * (nc + j) + 6] for j in range(Hc)]
    (wa, wup, wdn, vall, qvall, uball, vec, bias3, xin, cin, cb, xh1, rs1, a1, qkv, pt, o, h, xh2, rs2, a2, wot, wotp,
     gb, du, yacc, dacc, dout, a2t, ct, a1t, dwo, dxb, dubs, dqvs,
     sgs, sgc, sgp, sgz, sgr, sgf,
     lsem, osem, wsem, csem, rsem, vsem) = refs[6 * (nc + Hc):]
    H, T, W4 = C * Hc, NI * SP, 4 * E
    dp, row, col = Shift("dp", DP), Shift("row", R), Shift("col", C)
    d, r, c = dp.me, row.me, col.me
    sr, sl = split
    np_ = sr * sl
    part = np_ > 1

    loads = [pltpu.make_async_copy(x_hbm, xin, lsem.at[0]), pltpu.make_async_copy(c_hbm, cin, lsem.at[1])]
    own = pl.ds(pl.multiple_of(r * rows, rows), rows)
    heads = pl.ds(c * Hc, Hc)
    wloads = [pltpu.make_async_copy(aw_h, wa.at[heads, own, :], lsem.at[2]),
              pltpu.make_async_copy(up_h, wup.at[c, own, :], lsem.at[3]),
              pltpu.make_async_copy(dn_h, wdn.at[c, own, :], lsem.at[4])]
    for cp in loads + wloads:
        cp.start()
    for i, v in enumerate([g1_h, b1_h, ob_h, g2_h, b2_h, db_h]):
        vall[r, i:i + 1, 0:rows] = v[...].reshape(1, rows)
    qvall[c] = qvb_h[...]
    uball[c] = ub_h[...].reshape(1, FH)

    barrier = pltpu.get_barrier_semaphore()
    for ax in (dp, row, col):
        for k in ax.ks():
            pl.semaphore_signal(barrier, inc=1, device_id={ax.axis: ax.up(k)}, device_id_type=MESH)

    xh1[:, SP - 16:, :] = jnp.zeros((NI, 16, D), F32)
    h[:, SP - 16:, :] = jnp.zeros((NI, 16, D), F32)
    yacc[:, SP - 16:, :] = jnp.zeros((NI, 16, D), F32)
    rs1[:, SP - 16:, :] = jnp.zeros((NI, 16, 1), F32)
    sgs[...] = jnp.zeros(sgs.shape, F32)
    pl.semaphore_wait(barrier, (DP - 1) + (R - 1) + (C - 1))

    piece = d if part else 0
    off = lax.rem(c * Hc, 2)
    order = [lax.rem(off + e, Hc) for e in range(Hc)]
    units = [[(aw_h.at[j], wa.at[c * Hc + j])] for j in order]
    for lo, w in chunks:
        cut = (slice(None), pl.ds(lo, w))
        units.append([(up_h.at[cut], wup.at[(c,) + cut]), (dn_h.at[cut], wdn.at[(c,) + cut])])

    def cut_of(ref, rr, q):
        pr, pw = rows // sr, ref.shape[1] // sl
        return ref.at[pl.ds(pl.multiple_of(rr * rows + (q // sl) * pr, pr), pr),
                      pl.ds(pl.multiple_of(lax.rem(q, sl) * pw, pw), pw)]

    def gather_z(u):
        return [remote(cut_of(src, 0, piece), cut_of(dst, r, piece), wsem.at[0, 0, u], wsem.at[1, 0, u], "row", row.up(k))
                for src, dst in units[u] for k in row.ks()]

    def gather_p(u):
        out = []
        for _, dst in units[u] if part else ():
            for k in row.ks():
                b = cut_of(dst, row.down(k), piece)
                out += [remote(b, b, wsem.at[0, 1, u], wsem.at[1, 1, u], "dp", dp.up(kd)) for kd in dp.ks()]
        return out

    def gather_c(u):
        at = u if u < Hc else Hc + 2 * (u - Hc)
        return [remote(dst, dst, csem.at[0, at + i, k - 1], csem.at[1, at + i, k - 1], "col", col.up(k))
                for i, (_, dst) in enumerate(units[u]) for k in col.ks()]

    def settle_z(side, u):
        sb = (tbuf[u] if u < Hc else fbuf[u - Hc])[0]
        if R > 1:
            settle(wsem.at[side, 0, u], sb.at[0, 0, :, 0:R - 1])

    def settle_p(side, u):
        sb = (tbuf[u] if u < Hc else fbuf[u - Hc])[0]
        if R > 1 and part:
            settle(wsem.at[side, 1, u], sb.at[0, 0:DP - 1, :, 0:R - 1])

    def settle_c(side, u):
        for cp in gather_c(u):
            cp.wait_recv() if side else cp.wait_send()

    def begin(copies):
        for cp in copies:
            cp.start()

    U = Hc + nc
    for u in range(Hc):
        begin(gather_z(u))
    vz = [remote(vall.at[r], vall.at[r], vsem.at[0, 0], vsem.at[1, 0], "row", row.up(k)) for k in row.ks()]
    vc = [remote(qvall.at[c], qvall.at[c], vsem.at[0, 1], vsem.at[1, 1], "col", col.up(k)) for k in col.ks()]
    vc += [remote(uball.at[c], uball.at[c], vsem.at[0, 2], vsem.at[1, 2], "col", col.up(k)) for k in col.ks()]

    def settle_v(side):
        if R > 1:
            settle(vsem.at[side, 0], vall.at[0:R - 1])
        if C > 1:
            settle(vsem.at[side, 1], qvall.at[0:C - 1])
            settle(vsem.at[side, 2], uball.at[0:C - 1])

    def settle_g(side, stage):
        n, ref = ((C - 1, sgc), (DP - 1, sgp), (R - 1, sgr))[stage]
        if n:
            settle(vsem.at[side, 3 + stage], ref.at[0:n])

    begin(vz + vc)
    loads[0].wait()

    def norm1(i, carry):
        xf = xin[i].astype(F32)
        xh, rstd = norm_parts(xf)
        xh1[i, :SEQ] = xh
        rs1[i, :SEQ] = rstd
        h[i, :SEQ] = xf
        return carry

    loop(0, NI, norm1, 0)
    for u in range(Hc):
        settle_z(1, u)
        begin(gather_p(u))
    for u in range(Hc, U):
        begin(gather_z(u))
    loads[1].wait()

    def prep(i, carry):
        yacc[i, :SEQ] = cin[i].astype(F32)
        cb[i] = yacc[i].astype(BF16)
        return carry

    loop(0, NI, prep, 0)
    settle_v(1)
    vec[...] = jnp.concatenate([vall[rr][:, :rows] for rr in range(R)], axis=1)
    for hh in range(H):
        qb = qvall[hh // Hc][:, (hh % Hc) * E:(hh % Hc + 1) * E]
        zz = jnp.zeros((1, E), F32)
        bias3[hh] = jnp.concatenate([zz, qb[0:1], qb[1:2], zz], axis=1)

    def act1(i, carry):
        a1[i] = (xh1[i] * vec[0:1, :] + vec[1:2, :]).astype(BF16)
        return carry

    loop(0, NI, act1, 0)
    for cp in wloads:
        cp.wait()
    first = min(2, Hc)
    for u in range(first):
        settle_p(1, u)
        begin(gather_c(u))

    live = SEQ // 16 * 16
    key_ok = lax.broadcasted_iota(jnp.int32, (SP - live, SP), 0) < SEQ - live

    def logits(t):
        return mm(t[:, :E], t[:, E:2 * E], 1, 1)

    def attend(s, t):
        s = jnp.concatenate([s[:live], jnp.where(key_ok, s[live:], -1e30)], axis=0)
        top = jnp.max(s, 0, keepdims=True)
        e = jnp.exp2((s - top) * (LOG2E / math.sqrt(E)))
        return (e * (1.0 / rsum(e))).astype(BF16)

    def weigh(p, t):
        return mm(p, t[:, 2 * E:3 * E], 0, 0).astype(BF16)

    def fwd(it, carry):
        pr = lax.rem((c * Hc + 1) // 2 + it, H // 2)
        a = a1[...].reshape(T, D)
        ts = []
        for hh in (2 * pr, 2 * pr + 1):
            w = wa[hh]
            w = jnp.concatenate([w[:, E:2 * E], w[:, :E], w[:, 2 * E:]], axis=1)
            t = (mm(a, w, 1, 0) + bias3[hh]).astype(BF16)
            qkv[hh] = t.reshape(NI, SP, W4)
            ts.append(t)
        todo = [(i, j, ts[j][i * SP:(i + 1) * SP]) for i in range(NI) for j in range(2)]
        ahead, probs, outs = [logits(todo[0][2])], [], []

        def out(n):
            i, j, t = todo[n]
            outs.append(weigh(probs[n], t))
            if j == 1:
                o[i, :, pl.ds(pl.multiple_of(pr * 2 * E, 2 * E), 2 * E)] = jnp.concatenate(outs[-2:], axis=1)

        for n, (i, j, t) in enumerate(todo):
            if n + 1 < len(todo):
                ahead.append(logits(todo[n + 1][2]))
            probs.append(attend(ahead[n], t))
            pt[2 * pr + j, i] = probs[n]
            if n:
                out(n - 1)
        out(len(todo) - 1)
        return carry

    loop(0, 1, fwd, 0)
    for u in range(first, Hc):
        settle_p(1, u)
        begin(gather_c(u))
    for u in range(Hc, U):
        settle_z(1, u)
        begin(gather_p(u))
    ct[...] = cb[...].reshape(T, D).T
    a1t[:D] = a1[...].reshape(T, D).T
    a1t[D:] = jnp.ones((16, T), BF16)
    a2t[D:] = jnp.ones((16, T), BF16)
    for u in range(Hc):
        settle_c(1, u)
    loop(1, H // 2, fwd, 0)
    wot[...] = jnp.concatenate([wa[hh][:, 3 * E:] for hh in range(H)], axis=1)
    for hh in range(H):
        wotp[:, hh * 2 * E:(hh + 1) * 2 * E] = jnp.concatenate([wa[hh][:, 3 * E:], jnp.zeros((D, E), BF16)], axis=1)
    settle_p(1, Hc)
    begin(gather_c(Hc))

    G = 2 if NI % 2 == 0 else 1
    GT, B = G * SP, 16
    tiles = [(lo, min(B, SP - lo)) for lo in range(0, SP, B)]

    if "proj" not in SKIP:
        ms = [mm(o[0], wot[...], 1, 1)]
        for i in range(NI):
            if i + 1 < NI:
                ms.append(mm(o[i + 1], wot[...], 1, 1))
            for lo, n in tiles:
                rs = slice(lo, lo + n)
                hid = h[i, rs] + ms[i][rs] + vec[2:3, :]
                h[i, rs] = hid
                xh, rstd = norm_parts(hid)
                xh2[i, rs] = xh
                rs2[i, rs] = rstd
                a2[i, rs] = (xh * vec[3:4, :] + vec[4:5, :]).astype(BF16)
                yacc[i, rs] = hid + vec[5:6, :]
    a2t[:D] = a2[...].reshape(T, D).T

    ax = (dp, row, col)
    redf = [Reduce((rows, split), ax, fbuf[i], rsem.at[i], True) for i in range(nc)]
    redt = [Reduce((rows, split), ax, tbuf[j], rsem.at[nc + j], False) for j in range(Hc)]

    plan = {("f", 2): [(0, "q")], "mid": [(1, "q"), (2, "p"), (0, "z")], (1, 0): [(1, "z"), (2, "q")],
            (1, 1): [(0, "a")], (2, 0): [(2, "z")], (2, 1): [(3, "z")], "last": [(4, "z"), (1, "a")],
            "end": [(5, "z"), (2, "a"), (3, "a")], "end2": [(4, "a")], "end3": [(5, "a")]}
    reds = redf + redt
    if (nc, Hc, C) != (3, 3, 2):
        plan = {"mid": [(nc - 1, "p")], "last": [(u, "q") for u in range(nc + Hc)] + [(u, "z") for u in range(nc + Hc)],
                "end": [(u, "a") for u in range(nc + Hc)]}

    def step(at):
        for u, what in plan.get(at, ()):
            getattr(reds[u], "start_" + what)()

    def ff(half, lo, w, first):
        w1, w2 = wup.at[half, :, lo:lo + w], wdn.at[half, :, lo:lo + w]
        bias = uball[half, :, lo:lo + w]

        halves = [(k, min(256, w - k)) for k in range(0, w, 256)]
        todo = [(slice(i, i + G), k, m) for i in range(0, NI, G) for k, m in halves]

        def dots(n):
            im, k, m = todo[n]
            return (mm(a2[im].reshape(GT, D), w1[:, k:k + m], 1, 0), mm(cb[im].reshape(GT, D), w2[:, k:k + m], 1, 0))

        def down(im):
            yacc[im] += mm(gb[im, :, :w].reshape(GT, w), w2[...], 1, 1).reshape(G, SP, D)
            dd = mm(du[im, :, :w].reshape(GT, w), w1[...], 1, 1).reshape(G, SP, D)
            dacc[im] = dd if first else dacc[im] + dd

        if "ffone" not in SKIP:
            ahead = [dots(0)]
            for n, (im, k, m) in enumerate(todo):
                if n + 1 < len(todo):
                    ahead.append(dots(n + 1))
                u, dd = ahead[n]
                act, slope = gelu_parts(u + bias[:, k:k + m])
                gb[im, :, k:k + m] = act.astype(BF16).reshape(G, SP, m)
                du[im, :, k:k + m] = (dd * slope).astype(BF16).reshape(G, SP, m)
                if k == 0 and n:
                    down(todo[n - 1][0])
            down(todo[-1][0])
        gu = mm(a2t[...], du[:, :, :w].reshape(T, w), 1, 0)
        dubs[half, :, lo:lo + w] = gu[D:D + 1]
        return gu[:D], mm(ct[...], gb[:, :, :w].reshape(T, w), 1, 0)

    for i, (lo, w) in enumerate(chunks):
        for a, v in enumerate(ff(c, lo, w, i == 0)):
            redf[i].put(C - 1, a, v)
        if i:
            redf[i - 1].start_p()
        step(("f", i))
        if i + 1 < nc:
            settle_p(1, Hc + i + 1)
            begin(gather_c(Hc + i + 1))
        settle_c(1, Hc + i)
        for k in col.ks():
            for a, v in enumerate(ff(col.up(k), lo, w, False)):
                redf[i].put(k - 1, a, v)
            redf[i].c(k).start()

    z = jnp.zeros((8, D), F32)
    def dout_of(i):
        dd = mm(a2[i], wotp[...], 1, 0).astype(BF16)
        for hh in range(H):
            dout[hh, i] = dd[:, hh * 2 * E:(hh + 1) * 2 * E]

    sums = [z, z, z, z]
    for i in range(NI):
        xin[i] = yacc[i][:SEQ].astype(BF16)
        for lo, n in tiles:
            rs = slice(lo, lo + n)
            cf = cb[i, rs].astype(F32)
            da = dacc[i, rs]
            xh = xh2[i, rs]
            dh = cf + norm_back(da, vec[3:4, :], xh, rs2[i, rs])
            h[i, rs] = dh
            a2[i, rs] = dh.astype(BF16)
            sums = [t + fold(v) for t, v in zip(sums, (cf, da * xh, da, dh))]
        if i:
            dout_of(i - 1)
    dout_of(NI - 1)
    s_db, s_g2, s_b2, s_ob = (rsum(v) for v in sums)
    y_cp = pltpu.make_async_copy(xin, y_o, osem.at[0])
    y_cp.start()
    step("mid")
    ct[...] = a2[...].reshape(T, D).T
    dwo_all = mm(ct[...], o[...].reshape(T, D), 1, 0)
    for hh in range(H):
        dwo[hh] = jnp.concatenate([jnp.zeros((D, E), F32), dwo_all[:, hh * E:(hh + 1) * E]], axis=1)

    low = lax.broadcasted_iota(jnp.int32, (SP, 2 * E), 1) < E

    def back(hh):
        if "back" not in SKIP:
            def dprob(i):
                return mm(qkv[hh, i, :, 2 * E:] * (1.0 / math.sqrt(E)), dout[hh, i], 1, 1)

            def grads(i, p, ds):
                kq = qkv[hh, i, :, :2 * E]
                dv = mm(p, dout[hh, i], 1, 0)
                dk = mm(ds, kq, 1, 0)
                dq = mm(ds, kq, 0, 0)
                qkv[hh, i, :, :2 * E] = jnp.where(low, dq, dk).astype(BF16)
                qkv[hh, i, :, 2 * E:] = dv.astype(BF16)

            ahead, last_ = [dprob(0)], None
            for i in range(NI):
                if i + 1 < NI:
                    ahead.append(dprob(i + 1))
                dpr = ahead[i]
                p = pt[hh, i]
                pf = p.astype(F32)
                delta = rsum(pf * dpr)
                ds = (pf * (dpr - delta)).astype(BF16)
                if last_:
                    grads(*last_)
                last_ = (i, p, ds)
            grads(*last_)
        g = mm(a1t[...], qkv[hh].reshape(T, W4), 1, 0)
        dqvs[hh] = g[D:D + 1]
        return jnp.concatenate([g[:D, :2 * E], g[:D, 2 * E:] + dwo[hh]], axis=1)

    for j in range(Hc):
        def pair(s, carry):
            redt[j].put(s, 0, back(lax.rem(c + 1 + s, C) * Hc + j))

            @pl.when(s < C - 1)
            def _():
                redt[j].c(s + 1).start()
                step((j, 0))

            return carry

        lax.fori_loop(0, C, pair, 0)
        redt[j].start_p()
        step((j, 1))

    def da1(i):
        t = mm(qkv[0, i], wa[0], 1, 1)
        for hh in range(1, H):
            t = t + mm(qkv[hh, i], wa[hh], 1, 1)
        return t

    sums, ds = [z, z], [da1(0)]
    for i in range(NI):
        if i + 1 < NI:
            ds.append(da1(i + 1))
        for lo, n in tiles:
            rs = slice(lo, lo + n)
            da = ds[i][rs]
            xh = xh1[i, rs]
            dx = h[i, rs] + norm_back(da, vec[0:1, :], xh, rs1[i, rs])
            keep = min(n, SEQ - lo)
            dxb[i, lo:lo + keep] = dx[:keep]
            sums = [t + fold(v) for t, v in zip(sums, (da * xh, da))]
    s_g1, s_b1 = (rsum(v) for v in sums)
    dx_cp = pltpu.make_async_copy(dxb, dx_o, osem.at[1])
    dx_cp.start()

    six = jnp.concatenate([s_g1, s_b1, s_ob, s_g2, s_b2, s_db], axis=0)
    nf = FH // 128
    for cc in range(C):
        tail = [jnp.concatenate([dqvs[cc * Hc + j][:, :E], dqvs[cc * Hc + j][:, 2 * E:3 * E]], axis=1) for j in range(Hc)]
        tail += [dubs[cc][:, j * 128:(j + 1) * 128] for j in range(nf)]
        tail = jnp.concatenate(tail, axis=0)
        for rr in range(R):
            sgs[cc, rr, 0:6, 0:rows] = six[:, rr * rows:(rr + 1) * rows]
            sgs[cc, rr, 6:6 + Hc + nf, 0:128] = tail
    sgc[c] = sgs[c]
    gc = [remote(sgs.at[col.up(k)], sgc.at[c], vsem.at[0, 3], vsem.at[1, 3], "col", col.up(k)) for k in col.ks()]
    for cp in gc:
        cp.start()
    step("last")
    settle_g(1, 0)
    s = sgc[0]
    for k in range(1, C):
        s = s + sgc[k]
    sgp[d] = s
    gp = [remote(sgp.at[d], sgp.at[d], vsem.at[0, 4], vsem.at[1, 4], "dp", dp.up(k)) for k in dp.ks()]
    for cp in gp:
        cp.start()
    step("end")
    settle_g(1, 1)
    s = sgp[0]
    for k in range(1, DP):
        s = s + sgp[k]
    sgz[...] = s
    sgr[r] = sgz[r]
    gz = [remote(sgz.at[row.up(k)], sgr.at[r], vsem.at[0, 5], vsem.at[1, 5], "row", row.up(k)) for k in row.ks()]
    for cp in gz:
        cp.start()

    outs = [y_cp, dx_cp]
    step("end2")
    for i in range(nc):
        redf[i].finish()
        outs.append(pltpu.make_async_copy(redf[i].fin, ff_o[i], osem.at[3 + i]))
        outs[-1].start()
    step("end3")
    settle_g(1, 2)
    s = sgr[0]
    for k in range(1, R):
        s = s + sgr[k]
    sgf[...] = s
    outs.append(pltpu.make_async_copy(sgf, sg_o, osem.at[2]))
    outs[-1].start()
    for j in range(Hc):
        redt[j].finish()
        outs.append(pltpu.make_async_copy(redt[j].fin, ft_o.at[j], osem.at[3 + nc + j]))
        outs[-1].start()
    for red in redf + redt:
        red.drain()
    for u in range(U):
        settle_z(0, u)
        settle_p(0, u)
        settle_c(0, u)
    settle_v(0)
    for stage in range(3):
        settle_g(0, stage)
    for cp in outs:
        cp.wait()


def finish_kernel(cfg, *refs):
    rows, Hc, E, nf, (sr, sl), chunks = cfg
    nc = len(chunks)
    (y_i, dx_i, ft_i, sg_i), ff_i, refs = refs[:4], refs[4:4 + nc], refs[4 + nc:]
    (y_o, dx_o, dg1_o, db1_o, daw_o, dqvb_o, dob_o, dg2_o, db2_o, dup_o, dub_o, ddn_o, ddb_o) = refs[:13]
    (ybuf, xbuf, ft, sg, wf, wt, isem, osem), ff = refs[13:21], refs[21:]
    n = ybuf.shape[0]
    small = [pltpu.make_async_copy(i, v, isem.at[2 * n + k]) for k, (i, v) in enumerate(((sg_i, sg), (ft_i, ft), *zip(ff_i, ff)))]
    ins = [pltpu.make_async_copy(dx_i.at[k], xbuf.at[k], isem.at[k]) for k in range(n)]
    ins += [pltpu.make_async_copy(y_i.at[k], ybuf.at[k], isem.at[n + k]) for k in range(n)]
    outs = [pltpu.make_async_copy(xbuf.at[k], dx_o.at[k], osem.at[k]) for k in range(n)]
    outs += [pltpu.make_async_copy(ybuf.at[k], y_o.at[k], osem.at[n + k]) for k in range(n)]
    for cp in small + ins:
        cp.start()
    small[0].wait()
    s = sg[...]
    for i, ref in enumerate([dg1_o, db1_o, dob_o, dg2_o, db2_o, ddb_o]):
        ref[...] = s[i:i + 1, :rows].reshape(rows)
    for j in range(nf):
        dub_o[pl.ds(j * 128, 128)] = s[6 + Hc + j:7 + Hc + j, :128].reshape(128)
    for j in range(Hc):
        dqvb_o[0:1, j * E:(j + 1) * E] = s[6 + j:7 + j, :E]
        dqvb_o[1:2, j * E:(j + 1) * E] = s[6 + j:7 + j, E:2 * E]

    def lay(src, a, ref, lo):
        pr, pw = src.shape[-2:]
        for qr in range(sr):
            for ql in range(sl):
                ref[pl.ds(qr * pr, pr), pl.ds(lo + ql * pw, pw)] = src[qr * sl + ql, a].astype(F32)

    small[1].wait()
    for j in range(Hc):
        lay(ft.at[j], 0, wt.at[j], 0)
    for i, (lo, w) in enumerate(chunks):
        small[2 + i].wait()
        for a in range(2):
            lay(ff[i], a, wf.at[a], lo)
    big = [pltpu.make_async_copy(b, o, osem.at[2 * n + k]) for k, (b, o) in enumerate(((wf.at[0], dup_o), (wf.at[1], ddn_o), (wt, daw_o)))]
    for o in big:
        o.start()
    outs += big
    for i, o in zip(ins, outs):
        i.wait()
        o.start()
    for o in outs:
        o.wait()


def pick_split(n, rows, widths):
    for sr in range(1, n + 1):
        if n % sr == 0 and rows % (16 * sr) == 0 and all(w % (128 * (n // sr)) == 0 for w in widths):
            return sr, n // sr
    return 1, 1


def local(sizes, x, g1, b1, aw, qvb, ob, g2, b2, up, ub, dn, db, c):
    DP, R, C = sizes
    NI, SEQ, D = x.shape
    Hc, rows, W4 = aw.shape
    E, FH = W4 // 4, up.shape[1]
    H, SP = C * Hc, -(-SEQ // 16) * 16
    T = NI * SP
    chunks = tuple((lo, 256) for lo in range(0, FH, 256)) if FH % 256 == 0 else ((0, FH),)
    nc, wmax = len(chunks), max(w for _, w in chunks)
    split = pick_split(DP, rows, (W4,) + tuple(w for _, w in chunks))
    np_ = split[0] * split[1]
    pr, pw = rows // split[0], W4 // split[1]
    sd, vm = jax.ShapeDtypeStruct, pltpu.VMEM
    dma = pltpu.SemaphoreType.DMA
    nf, VW = FH // 128, -(-rows // 128) * 128
    S = -(-(6 + Hc + nf) // 8) * 8
    cfg = (DP, R, C, NI, SEQ, SP, D, Hc, E, FH, rows, split, chunks)

    def red(A, L):
        pw = L // split[1]
        return [vm((C, np_, A, R, pr, pw), BF16), vm((max(C - 1, 1), np_, A, R, pr, pw), BF16), vm((DP, A, R, pr, pw), BF16),
                vm((R, A, pr, pw), BF16), vm((R, A, pr, pw), BF16), vm((np_, A, pr, pw), BF16)]

    scratch = sum([red(2, w) for _, w in chunks] + [red(1, W4)] * Hc, []) + [
        vm((H, D, W4), BF16), vm((C, D, FH), BF16), vm((C, D, FH), BF16), vm((R, 8, VW), F32),
        vm((C, 2, Hc * E), F32), vm((C, 1, FH), F32), vm((8, D), F32), vm((H, 1, W4), F32),
        vm((NI, SEQ, D), BF16), vm((NI, SEQ, D), BF16), vm((NI, SP, D), BF16), vm((NI, SP, D), F32), vm((NI, SP, 1), F32),
        vm((NI, SP, D), BF16), vm((H, NI, SP, W4), BF16), vm((H, NI, SP, SP), BF16), vm((NI, SP, D), BF16),
        vm((NI, SP, D), F32), vm((NI, SP, D), F32), vm((NI, SP, 1), F32), vm((NI, SP, D), BF16), vm((D, D), BF16),
        vm((D, 2 * D), BF16),
        vm((NI, SP, wmax), BF16), vm((NI, SP, wmax), BF16), vm((NI, SP, D), F32), vm((NI, SP, D), F32),
        vm((H, NI, SP, 2 * E), BF16), vm((D + 16, T), BF16), vm((D, T), BF16), vm((D + 16, T), BF16),
        vm((H, D, 2 * E), F32), vm((NI, SEQ, D), F32), vm((C, 1, FH), F32), vm((H, 1, W4), F32),
        vm((C, R, S, VW), F32), vm((C, R, S, VW), F32), vm((DP, R, S, VW), F32), vm((R, S, VW), F32),
        vm((R, S, VW), F32), vm((S, VW), F32),
        dma((5,)), dma((3 + nc + Hc,)), dma((2, 2, Hc + nc)), dma((2, Hc + 2 * nc, max(C - 1, 1))), dma((nc + Hc, 2, 5)), dma((2, 6)),
    ]
    any_ = pl.BlockSpec(memory_space=pl.ANY)
    vm_ = pl.BlockSpec(memory_space=pltpu.VMEM)
    v = lambda a: sd(a.shape, F32)
    y, dx, ft, sg, *ff = pl.pallas_call(
        functools.partial(kernel, cfg),
        out_shape=(sd(x.shape, BF16), v(x), sd((Hc, np_, 1, pr, pw), BF16), sd((S, VW), F32),
                   *[sd((np_, 2, pr, w // split[1]), BF16) for _, w in chunks]),
        in_specs=[any_, vm_, vm_, any_, vm_, vm_, vm_, vm_, any_, vm_, any_, vm_, any_],
        out_specs=[any_] * (4 + nc),
        scratch_shapes=scratch,
        compiler_params=pltpu.CompilerParams(vmem_limit_bytes=67043328, collective_id=0, has_side_effects=True),
    )(x, g1, b1, aw, qvb, ob, g2, b2, up, ub, dn, db, c)
    return tuple(pl.pallas_call(
        functools.partial(finish_kernel, (rows, Hc, E, nf, split, chunks)),
        out_shape=(sd(x.shape, BF16), v(x), v(g1), v(b1), v(aw), v(qvb), v(ob), v(g2), v(b2), v(up), v(ub), v(dn), v(db)),
        in_specs=[any_] * (4 + nc),
        out_specs=[any_, any_, vm_, vm_, any_, vm_, vm_, vm_, vm_, any_, vm_, any_, vm_],
        scratch_shapes=[vm(x.shape, BF16), vm(x.shape, F32), vm(ft.shape, BF16), vm(sg.shape, F32),
                        vm((2, rows, FH), F32), vm(aw.shape, F32), dma((2 * NI + 2 + nc,)), dma((2 * NI + 3,)),
                        *[vm(f.shape, BF16) for f in ff]],
        compiler_params=pltpu.CompilerParams(vmem_limit_bytes=67043328),
    )(y, dx, ft, sg, *ff))


def solution(mesh):
    sizes = tuple(mesh.shape[a] for a in ("dp", "row", "col"))
    placed = (
        P(("dp", "row", "col"), None, None),
        P("row"),
        P("row"),
        P("col", "row", None),
        P(None, "col"),
        P("row"),
        P("row"),
        P("row"),
        P("row", "col"),
        P("col"),
        P("row", "col"),
        P("row"),
        P(("dp", "row", "col"), None, None),
    )
    return jax.shard_map(
        functools.partial(local, sizes),
        mesh=mesh,
        in_specs=placed,
        out_specs=(
            P(("dp", "row", "col"), None, None),
            P(("dp", "row", "col"), None, None),
            P("row"),
            P("row"),
            P("col", "row", None),
            P(None, "col"),
            P("row"),
            P("row"),
            P("row"),
            P("row", "col"),
            P("col"),
            P("row", "col"),
            P("row"),
        ),
        check_vma=False,
    )
```

time: 83.7 us -> 70.3 us (0.84)
  Pallas kernels: 82.6 us -> 69.3 us
    pallas_call x1, Pallas kernels: 78.8 us -> 65.5 us  [local(): pl.pallas_call(functools.partial(kernel, cfg), out_shape=(sd(x.shape, BF1...]
where the time goes in v4:
time: 70.3 us; the launch traced here: 70.1 us
  Pallas kernels  69.3 us (99%)
  between operations  0.84 us (1%)
    pallas_call x1, Pallas kernels, local(): pl.pallas_call(functools.partial(kernel, cfg), out_shape=(sd(x.shape, BF1...  65.5 us
    pallas_call x1, Pallas kernels, local(): pl.pallas_call(functools.partial(finish_kernel, (rows, Hc, E, nf, split,...  3.8 us

profile of v4, /device:TPU:0, one launch (start us, length us, event | category | flops | bytes accessed | tf_op | source)
XLA Modules:
  0.0 70.1 jit_solution(11292178715588764200)
XLA Ops:
  0.6 65.5 %shard_map.228 = (bf16[6,197,384]{2,1,0:T(8,128)(2,1)}, f32[6,197,384]{2,1,0:T(8,128)}, bf16[3,4,1,48,128]{4,3,2,1,0:T(8,128)(2,1)}, f32[16,128]{1,0:T(8,128)}, ...) custom-call(bf16[6,197,384]{2,1,0:T(8,128)(2,1)} %refs_0_.1, ...), custom_call_target="tpu_custom_call" | custom-call | tf_op jit(solution)/shard_map/pallas_call | solution.py:771
  66.2 3.8 %shard_map.229 = (bf16[6,197,384]{2,1,0:T(8,128)(2,1)}, f32[6,197,384]{2,1,0:T(8,128)}, f32[96]{0:T(128)}, f32[96]{0:T(128)}, f32[3,96,256]{2,1,0:T(8,128)}, /*i...) custom-call(bf16[6,197,384]{2,1,0:T(8,128)(2,1)} %get-tuple-element., ...), custom_call_target="tpu_custom_call" | custom-call | tf_op jit(solution)/shard_map/pallas_call | solution.py:780

commit v5 on v4

--- a/solution.py
+++ b/solution.py
@@ -39,11 +39,11 @@
     return u * cdf, cdf + (w * bell) * (INV_ROOT_TWO_PI / ROOT_HALF)
 
 
-SKIP = set()
-
-
-def loop(lo, hi, body, init, **kw):
-    return init if body.__name__ in SKIP else lax.fori_loop(lo, hi, body, init, **kw)
+DEEP = (3, 2, 3)
+
+
+def loop(lo, hi, body, init):
+    return lax.fori_loop(lo, hi, body, init)
 
 
 def rsum(v):
@@ -376,35 +376,38 @@
         return (e * (1.0 / rsum(e))).astype(BF16)
 
     def weigh(p, t):
-        return mm(p, t[:, 2 * E:3 * E], 0, 0).astype(BF16)
+        return mm(t[:, 2 * E:].T[:E], p, 1, 0)
 
     def fwd(it, carry):
         pr = lax.rem((c * Hc + 1) // 2 + it, H // 2)
-        a = a1[...].reshape(T, D)
-        ts = []
-        for hh in (2 * pr, 2 * pr + 1):
-            w = wa[hh]
+        todo = [(i, j) for i in range(NI) for j in range(2)]
+        N, ts, vts, ahead, probs, outs = len(todo), [], [], [], [], []
+
+        def project(n):
+            i, j = todo[n]
+            w = wa[2 * pr + j]
             w = jnp.concatenate([w[:, E:2 * E], w[:, :E], w[:, 2 * E:]], axis=1)
-            t = (mm(a, w, 1, 0) + bias3[hh]).astype(BF16)
-            qkv[hh] = t.reshape(NI, SP, W4)
+            t = (mm(a1[i], w, 1, 0) + bias3[2 * pr + j]).astype(BF16)
+            qkv[2 * pr + j, i] = t
             ts.append(t)
-        todo = [(i, j, ts[j][i * SP:(i + 1) * SP]) for i in range(NI) for j in range(2)]
-        ahead, probs, outs = [logits(todo[0][2])], [], []
+            vts.append(t[:, 2 * E:].T[:E])
 
         def out(n):
-            i, j, t = todo[n]
-            outs.append(weigh(probs[n], t))
+            i, j = todo[n]
+            outs.append(mm(vts[n], probs[n], 1, 0))
             if j == 1:
-                o[i, :, pl.ds(pl.multiple_of(pr * 2 * E, 2 * E), 2 * E)] = jnp.concatenate(outs[-2:], axis=1)
-
-        for n, (i, j, t) in enumerate(todo):
-            if n + 1 < len(todo):
-                ahead.append(logits(todo[n + 1][2]))
-            probs.append(attend(ahead[n], t))
-            pt[2 * pr + j, i] = probs[n]
-            if n:
+                o[i, :, pl.ds(pl.multiple_of(pr * 2 * E, 2 * E), 2 * E)] = jnp.concatenate(outs[-2:], axis=0).astype(BF16).T
+
+        for n in range(-DEEP[0], N + 1):
+            if 0 <= n + DEEP[0] < N:
+                project(n + DEEP[0])
+            if 0 <= n + DEEP[1] < N:
+                ahead.append(logits(ts[n + DEEP[1]]))
+            if 0 <= n < N:
+                probs.append(attend(ahead[n], ts[n]))
+                pt[2 * pr + todo[n][1], todo[n][0]] = probs[n]
+            if n >= 1:
                 out(n - 1)
-        out(len(todo) - 1)
         return carry
 
     loop(0, 1, fwd, 0)
@@ -431,7 +434,7 @@
     GT, B = G * SP, 16
     tiles = [(lo, min(B, SP - lo)) for lo in range(0, SP, B)]
 
-    if "proj" not in SKIP:
+    if True:
         ms = [mm(o[0], wot[...], 1, 1)]
         for i in range(NI):
             if i + 1 < NI:
@@ -451,8 +454,8 @@
     redf = [Reduce((rows, split), ax, fbuf[i], rsem.at[i], True) for i in range(nc)]
     redt = [Reduce((rows, split), ax, tbuf[j], rsem.at[nc + j], False) for j in range(Hc)]
 
-    plan = {("f", 2): [(0, "q")], "mid": [(1, "q"), (2, "p"), (0, "z")], (1, 0): [(1, "z"), (2, "q")],
-            (1, 1): [(0, "a")], (2, 0): [(2, "z")], (2, 1): [(3, "z")], "last": [(4, "z"), (1, "a")],
+    plan = {("f", 2): [(0, "q")], "mid": [(1, "q"), (2, "p"), (0, "z")], (0, 1): [(1, "z")], (1, 0): [(2, "q")],
+            (2, 0): [(0, "a")], (2, 1): [(2, "z"), (3, "z")], "last": [(4, "z"), (1, "a")],
             "end": [(5, "z"), (2, "a"), (3, "a")], "end2": [(4, "a")], "end3": [(5, "a")]}
     reds = redf + redt
     if (nc, Hc, C) != (3, 3, 2):
@@ -475,25 +478,24 @@
             return (mm(a2[im].reshape(GT, D), w1[:, k:k + m], 1, 0), mm(cb[im].reshape(GT, D), w2[:, k:k + m], 1, 0))
 
         def down(im):
-            yacc[im] += mm(gb[im, :, :w].reshape(GT, w), w2[...], 1, 1).reshape(G, SP, D)
             dd = mm(du[im, :, :w].reshape(GT, w), w1[...], 1, 1).reshape(G, SP, D)
             dacc[im] = dd if first else dacc[im] + dd
 
-        if "ffone" not in SKIP:
+        if True:
             ahead = [dots(0)]
             for n, (im, k, m) in enumerate(todo):
                 if n + 1 < len(todo):
                     ahead.append(dots(n + 1))
                 u, dd = ahead[n]
                 act, slope = gelu_parts(u + bias[:, k:k + m])
-                gb[im, :, k:k + m] = act.astype(BF16).reshape(G, SP, m)
+                gb[half, im, :, lo + k:lo + k + m] = act.astype(BF16).reshape(G, SP, m)
                 du[im, :, k:k + m] = (dd * slope).astype(BF16).reshape(G, SP, m)
                 if k == 0 and n:
                     down(todo[n - 1][0])
             down(todo[-1][0])
         gu = mm(a2t[...], du[:, :, :w].reshape(T, w), 1, 0)
         dubs[half, :, lo:lo + w] = gu[D:D + 1]
-        return gu[:D], mm(ct[...], gb[:, :, :w].reshape(T, w), 1, 0)
+        return gu[:D], mm(ct[...], gb[half, :, :, lo:lo + w].reshape(T, w), 1, 0)
 
     for i, (lo, w) in enumerate(chunks):
         for a, v in enumerate(ff(c, lo, w, i == 0)):
@@ -518,7 +520,6 @@
 
     sums = [z, z, z, z]
     for i in range(NI):
-        xin[i] = yacc[i][:SEQ].astype(BF16)
         for lo, n in tiles:
             rs = slice(lo, lo + n)
             cf = cb[i, rs].astype(F32)
@@ -532,42 +533,37 @@
             dout_of(i - 1)
     dout_of(NI - 1)
     s_db, s_g2, s_b2, s_ob = (rsum(v) for v in sums)
-    y_cp = pltpu.make_async_copy(xin, y_o, osem.at[0])
-    y_cp.start()
     step("mid")
     ct[...] = a2[...].reshape(T, D).T
     dwo_all = mm(ct[...], o[...].reshape(T, D), 1, 0)
     for hh in range(H):
         dwo[hh] = jnp.concatenate([jnp.zeros((D, E), F32), dwo_all[:, hh * E:(hh + 1) * E]], axis=1)
 
-    low = lax.broadcasted_iota(jnp.int32, (SP, 2 * E), 1) < E
-
     def back(hh):
-        if "back" not in SKIP:
+        if True:
             def dprob(i):
                 return mm(qkv[hh, i, :, 2 * E:] * (1.0 / math.sqrt(E)), dout[hh, i], 1, 1)
 
-            def grads(i, p, ds):
-                kq = qkv[hh, i, :, :2 * E]
-                dv = mm(p, dout[hh, i], 1, 0)
-                dk = mm(ds, kq, 1, 0)
-                dq = mm(ds, kq, 0, 0)
-                qkv[hh, i, :, :2 * E] = jnp.where(low, dq, dk).astype(BF16)
-                qkv[hh, i, :, 2 * E:] = dv.astype(BF16)
-
-            ahead, last_ = [dprob(0)], None
-            for i in range(NI):
-                if i + 1 < NI:
-                    ahead.append(dprob(i + 1))
-                dpr = ahead[i]
-                p = pt[hh, i]
-                pf = p.astype(F32)
-                delta = rsum(pf * dpr)
-                ds = (pf * (dpr - delta)).astype(BF16)
-                if last_:
-                    grads(*last_)
-                last_ = (i, p, ds)
-            grads(*last_)
+            def turned(i):
+                return qkv[hh, i, :, :2 * E].T, dout[hh, i].T[:E]
+
+            def grads(i, p, ds, kqt, dot):
+                dq, dk, dv = mm(kqt[:E], ds, 1, 0), mm(kqt[E:], ds, 1, 1), mm(dot, p, 1, 1)
+                qkv[hh, i, :, :2 * E] = jnp.concatenate([dq, dk], axis=0).astype(BF16).T
+                qkv[hh, i, :, 2 * E:] = jnp.concatenate([dv, jnp.zeros((E, SP), F32)], axis=0).astype(BF16).T
+
+            ahead, done = [], []
+            for n in range(-DEEP[2], NI + 1):
+                if 0 <= n + DEEP[2] < NI:
+                    ahead.append((dprob(n + DEEP[2]), turned(n + DEEP[2])))
+                if 0 <= n < NI:
+                    dpr, ts = ahead[n]
+                    p = pt[hh, n]
+                    pf = p.astype(F32)
+                    delta = rsum(pf * dpr)
+                    done.append((n, p, (pf * (dpr - delta)).astype(BF16), *ts))
+                if n >= 1:
+                    grads(*done[n - 1])
         g = mm(a1t[...], qkv[hh].reshape(T, W4), 1, 0)
         dqvs[hh] = g[D:D + 1]
         return jnp.concatenate([g[:D, :2 * E], g[:D, 2 * E:] + dwo[hh]], axis=1)
@@ -627,19 +623,26 @@
     s = sgc[0]
     for k in range(1, C):
         s = s + sgc[k]
-    sgp[d] = s
-    gp = [remote(sgp.at[d], sgp.at[d], vsem.at[0, 4], vsem.at[1, 4], "dp", dp.up(k)) for k in dp.ks()]
-    for cp in gp:
-        cp.start()
-    step("end")
-    settle_g(1, 1)
-    s = sgp[0]
-    for k in range(1, DP):
-        s = s + sgp[k]
     sgz[...] = s
     sgr[r] = sgz[r]
     gz = [remote(sgz.at[row.up(k)], sgr.at[r], vsem.at[0, 5], vsem.at[1, 5], "row", row.up(k)) for k in row.ks()]
     for cp in gz:
+        cp.start()
+    step("end")
+    for i in range(NI):
+        t = yacc[i]
+        for k in range(C):
+            t = t + mm(gb[k, i], wdn[k], 1, 1)
+        xin[i] = t[:SEQ].astype(BF16)
+    y_cp = pltpu.make_async_copy(xin, y_o, osem.at[0])
+    y_cp.start()
+    settle_g(1, 2)
+    s = sgr[0]
+    for k in range(1, R):
+        s = s + sgr[k]
+    sgp[d] = s
+    gp = [remote(sgp.at[d], sgp.at[d], vsem.at[0, 4], vsem.at[1, 4], "dp", dp.up(k)) for k in dp.ks()]
+    for cp in gp:
         cp.start()
 
     outs = [y_cp, dx_cp]
@@ -649,10 +652,10 @@
         outs.append(pltpu.make_async_copy(redf[i].fin, ff_o[i], osem.at[3 + i]))
         outs[-1].start()
     step("end3")
-    settle_g(1, 2)
-    s = sgr[0]
-    for k in range(1, R):
-        s = s + sgr[k]
+    settle_g(1, 1)
+    s = sgp[0]
+    for k in range(1, DP):
+        s = s + sgp[k]
     sgf[...] = s
     outs.append(pltpu.make_async_copy(sgf, sg_o, osem.at[2]))
     outs[-1].start()
@@ -758,10 +761,10 @@
         vm((NI, SP, D), BF16), vm((H, NI, SP, W4), BF16), vm((H, NI, SP, SP), BF16), vm((NI, SP, D), BF16),
         vm((NI, SP, D), F32), vm((NI, SP, D), F32), vm((NI, SP, 1), F32), vm((NI, SP, D), BF16), vm((D, D), BF16),
         vm((D, 2 * D), BF16),
-        vm((NI, SP, wmax), BF16), vm((NI, SP, wmax), BF16), vm((NI, SP, D), F32), vm((NI, SP, D), F32),
+        vm((C, NI, SP, FH), BF16), vm((NI, SP, wmax), BF16), vm((NI, SP, D), F32), vm((NI, SP, D), F32),
         vm((H, NI, SP, 2 * E), BF16), vm((D + 16, T), BF16), vm((D, T), BF16), vm((D + 16, T), BF16),
         vm((H, D, 2 * E), F32), vm((NI, SEQ, D), F32), vm((C, 1, FH), F32), vm((H, 1, W4), F32),
-        vm((C, R, S, VW), F32), vm((C, R, S, VW), F32), vm((DP, R, S, VW), F32), vm((R, S, VW), F32),
+        vm((C, R, S, VW), F32), vm((C, R, S, VW), F32), vm((DP, S, VW), F32), vm((R, S, VW), F32),
         vm((R, S, VW), F32), vm((S, VW), F32),
         dma((5,)), dma((3 + nc + Hc,)), dma((2, 2, Hc + nc)), dma((2, Hc + 2 * nc, max(C - 1, 1))), dma((nc + Hc, 2, 5)), dma((2, 6)),
     ]

time: 70.3 us -> 68.3 us (0.972)
  Pallas kernels: 69.3 us -> 67.2 us
    pallas_call x1, Pallas kernels: 65.5 us -> 63.4 us  [local(): pl.pallas_call(functools.partial(kernel, cfg), out_shape=(sd(x.shape, BF1...]
where the time goes in v5:
time: 68.3 us; the launch traced here: 68 us
  Pallas kernels  67.2 us (98%)
  between operations  0.84 us (1%)
    pallas_call x1, Pallas kernels, local(): pl.pallas_call(functools.partial(kernel, cfg), out_shape=(sd(x.shape, BF1...  63.4 us
    pallas_call x1, Pallas kernels, local(): pl.pallas_call(functools.partial(finish_kernel, (rows, Hc, E, nf, split,...  3.8 us

profile of v5, /device:TPU:0, one launch (start us, length us, event | category | flops | bytes accessed | tf_op | source)
XLA Modules:
  0.0 68.0 jit_solution(4862547076780485779)
XLA Ops:
  0.6 63.4 %shard_map.228 = (bf16[6,197,384]{2,1,0:T(8,128)(2,1)}, f32[6,197,384]{2,1,0:T(8,128)}, bf16[3,4,1,48,128]{4,3,2,1,0:T(8,128)(2,1)}, f32[16,128]{1,0:T(8,128)}, ...) custom-call(bf16[6,197,384]{2,1,0:T(8,128)(2,1)} %refs_0_.1, ...), custom_call_target="tpu_custom_call" | custom-call | tf_op jit(solution)/shard_map/pallas_call | solution.py:774
  64.1 3.8 %shard_map.229 = (bf16[6,197,384]{2,1,0:T(8,128)(2,1)}, f32[6,197,384]{2,1,0:T(8,128)}, f32[96]{0:T(128)}, f32[96]{0:T(128)}, f32[3,96,256]{2,1,0:T(8,128)}, /*i...) custom-call(bf16[6,197,384]{2,1,0:T(8,128)(2,1)} %get-tuple-element., ...), custom_call_target="tpu_custom_call" | custom-call | tf_op jit(solution)/shard_map/pallas_call | solution.py:783

commit v6 on v5

--- a/solution.py
+++ b/solution.py
@@ -688,8 +688,11 @@
     ins += [pltpu.make_async_copy(y_i.at[k], ybuf.at[k], isem.at[n + k]) for k in range(n)]
     outs = [pltpu.make_async_copy(xbuf.at[k], dx_o.at[k], osem.at[k]) for k in range(n)]
     outs += [pltpu.make_async_copy(ybuf.at[k], y_o.at[k], osem.at[n + k]) for k in range(n)]
-    for cp in small + ins:
+    for cp in ins + small:
         cp.start()
+    for i, o in zip(ins, outs):
+        i.wait()
+        o.start()
     small[0].wait()
     s = sg[...]
     for i, ref in enumerate([dg1_o, db1_o, dob_o, dg2_o, db2_o, ddb_o]):
@@ -717,9 +720,6 @@
     for o in big:
         o.start()
     outs += big
-    for i, o in zip(ins, outs):
-        i.wait()
-        o.start()
     for o in outs:
         o.wait()
 

time: 68.3 us -> 68.1 us (level)
  no operation moved by 1% of the time
where the time goes in v6:
time: 68.1 us; the launch traced here: 67.9 us
  Pallas kernels  67.1 us (99%)
  between operations  0.84 us (1%)
    pallas_call x1, Pallas kernels, local(): pl.pallas_call(functools.partial(kernel, cfg), out_shape=(sd(x.shape, BF1...  63.4 us
    pallas_call x1, Pallas kernels, local(): pl.pallas_call(functools.partial(finish_kernel, (rows, Hc, E, nf, split,...  3.68 us

profile of v6, /device:TPU:0, one launch (start us, length us, event | category | flops | bytes accessed | tf_op | source)
XLA Modules:
  0.0 67.9 jit_solution(6949108571713652839)
XLA Ops:
  0.6 63.4 %shard_map.228 = (bf16[6,197,384]{2,1,0:T(8,128)(2,1)}, f32[6,197,384]{2,1,0:T(8,128)}, bf16[3,4,1,48,128]{4,3,2,1,0:T(8,128)(2,1)}, f32[16,128]{1,0:T(8,128)}, ...) custom-call(bf16[6,197,384]{2,1,0:T(8,128)(2,1)} %refs_0_.1, ...), custom_call_target="tpu_custom_call" | custom-call | tf_op jit(solution)/shard_map/pallas_call | solution.py:774
  64.1 3.7 %shard_map.229 = (bf16[6,197,384]{2,1,0:T(8,128)(2,1)}, f32[6,197,384]{2,1,0:T(8,128)}, f32[96]{0:T(128)}, f32[96]{0:T(128)}, f32[3,96,256]{2,1,0:T(8,128)}, /*i...) custom-call(bf16[6,197,384]{2,1,0:T(8,128)(2,1)} %get-tuple-element., ...), custom_call_target="tpu_custom_call" | custom-call | tf_op jit(solution)/shard_map/pallas_call | solution.py:783
